TPU v7x, 8 devices: a whole 2x2x1 slice. The times are simulated.
8 devices in a mesh: dp: 1 (over z), tp: 8 (over y, x, core).
Axes of the slice: x: 2, y: 2, z: 1, core: 2. Of those that a mesh axis runs over, the one named last changes fastest.
Arguments:
- x_rows: bfloat16 [8192, 2304], P(('dp', 'tp'))
- norm_gain: float32 [2304], replicated
- w_q: bfloat16 [2304, 8, 256], P(None, 'tp')
- w_k: bfloat16 [2304, 1024], P(None, 'tp')
- w_v: bfloat16 [2304, 1024], P(None, 'tp')
Outputs:
- output 1: bfloat16 [8192, 8, 256], P('dp', 'tp')
- output 2: bfloat16 [8192, 8, 256], P('dp', 'tp')
- output 3: bfloat16 [8192, 8, 256], P('dp', 'tp')
All inputs are finite; a program needn't handle non-finite values.
Results may differ from a plain program's by a relative error of at most 0.001.
Values are sent between devices in bfloat16 or wider.
A program may use at most 1 GiB of HBM per device.

v0:
```python
import jax
import jax.numpy as jnp
from jax import lax
from jax.sharding import PartitionSpec as P

EPSILON = 1e-6


def solution(mesh):
    group_size = mesh.shape["tp"]

    def head_pieces(piece, head_share):
        member = lax.axis_index("tp") % head_share
        received = [piece]
        for step_ahead in range(1, head_share):
            send_pairs = [(source, (source // head_share) * head_share + (source % head_share - step_ahead) % head_share) for source in range(group_size)]
            received.append(lax.ppermute(piece, "tp", send_pairs))
        joined = jnp.concatenate(received, axis=1)
        return jnp.roll(joined, member * piece.shape[1], axis=1)

    def local_step(x_rows, norm_gain, w_q, w_k, w_v):
        x_wide = x_rows.astype(jnp.float32)
        mean_sq = jnp.mean(x_wide * x_wide, axis=-1, keepdims=True)
        normed = (x_wide * lax.rsqrt(mean_sq + EPSILON) * norm_gain).astype(jnp.bfloat16)
        gathered = lax.all_gather(normed, "tp", axis=0, tiled=True)
        q_local = jnp.einsum("td,dhe->the", gathered, w_q, preferred_element_type=jnp.float32).astype(jnp.bfloat16)
        k_piece = jnp.dot(gathered, w_k, preferred_element_type=jnp.float32).astype(jnp.bfloat16)
        v_piece = jnp.dot(gathered, w_v, preferred_element_type=jnp.float32).astype(jnp.bfloat16)
        head_share = w_q.shape[2] // w_k.shape[1]
        k_head = head_pieces(k_piece, head_share)
        v_head = head_pieces(v_piece, head_share)
        return q_local, k_head[:, None, :], v_head[:, None, :]

    return jax.shard_map(local_step, mesh=mesh, in_specs=(P(("dp", "tp"), None), P(None), P(None, "tp", None), P(None, "tp"), P(None, "tp")), out_specs=(P("dp", "tp", None), P("dp", "tp", None), P("dp", "tp", None)), check_vma=False)
```

profile of v0, /device:TPU:1, one launch (start us, length us, event | category | flops | bytes accessed | tf_op | source)
XLA Modules:
  0.0 284.4 jit_solution(9844188463131622152)
XLA Ops:
  7.2 0.0 copy-start
  7.2 0.0 copy-start.1
  7.2 0.0 all-gather.2.cloned.1.call-start
  7.2 3.5 %fusion.1 = f32[1024]{0:T(1024)S(1)} fusion(bf16[1024,2304]{1,0:T(8,128)(2,1)} %param.7), kind=kLoop, calls=%fused_computation.6 | loop fusion | flops 7076864 | bytes 4722688 | tf_op jit(solution)/shard_map/reduce_sum | solution.py:23
  10.7 5.6 %fusion.3 = bf16[1024,2304]{1,0:T(8,128)(2,1)} fusion(bf16[1024,2304]{1,0:T(8,128)(2,1)} %param.7, f32[2304]{0:T(1024)} %param.8, f32[1024]{0:T(1024)S(1)} %add_rsqrt_fusion), kind=kLoop, calls=%fused_computation.8 | loop fusion | flops 9437184 | bytes 9450496 | tf_op jit(solution)/shard_map/convert_element_type | solution.py:24
  16.3 0.0 all-gather.2.cloned.1.call-update
  16.4 176.3 %all-gather.2.cloned.1.call-done = bf16[8192,2304]{1,0:T(8,128)(2,1)} async-done(((bf16[1024,2304]{1,0:T(8,128)(2,1)}), bf16[8192,2304]{1,0:T(8,128)(2,1)}) %all-gather.2.cloned.1.call-update) | async-done | bytes 37748752 | tf_op jit(solution)/shard_map/all_gather | solution.py:25
  192.7 0.0 copy-done.1
  192.7 19.2 %convolution_convert_fusion.2 = bf16[8192,128]{0,1:T(8,128)(2,1)} fusion(bf16[8192,2304]{1,0:T(8,128)(2,1)} %all-gather.2.cloned.1.call-done, bf16[2304,128]{1,0:T(8,128)(2,1)S(1)} %copy-done.1), kind=kOutput, calls=%fused_computation.5 | convolution fusion | flops 4832886784 | bytes 40435712 | tf_op jit(solution)/shard_map/dot_general | solution.py:27
  212.0 0.3 collective-permute-start
  212.2 17.9 %convolution_convert_fusion.1 = bf16[8192,128]{0,1:T(8,128)(2,1)S(1)} fusion(bf16[8192,2304]{1,0:T(8,128)(2,1)} %all-gather.2.cloned.1.call-done, bf16[2304,128]{1,0:T(8,128)(2,1)} %param.11), kind=kOutput, calls=%fused_computation.4 | convolution fusion | flops 4832886784 | bytes 40435712 | tf_op jit(solution)/shard_map/dot_general | solution.py:28
  230.2 0.3 collective-permute-start.1
  230.4 0.0 copy-done
  230.5 18.6 %fusion = bf16[8192,1,256]{2,0,1:T(8,128)(2,1)} fusion(bf16[8192,2304]{1,0:T(8,128)(2,1)} %all-gather.2.cloned.1.call-done, bf16[2304,1,256]{2,0,1:T(8,128)(2,1)S(1)} %copy-done), kind=kOutput, calls=%fused_computation.3 | convolution fusion | flops 9665773568 | bytes 43122688 | tf_op jit(solution)/shard_map/td,dhe->the/dot_general | solution.py:26
  249.1 0.0 collective-permute-done
  249.1 7.9 %fusion.8 = bf16[8192,256]{0,1:T(8,128)(2,1)} fusion(s32[]{:T(128)S(6)} %select_n.22, bf16[8192,128]{0,1:T(8,128)(2,1)} %convolution_convert_fusion.2, bf16[8192,128]{0,1:T(8,128)(2,1)} %collective-permute-done), kind=kLoop, calls=%fused_computation.21 | loop fusion | flops 16777216 | bytes 8388612 | tf_op jit(solution)/shard_map/jit(_roll_dynamic)/concatenate | solution.py:19
  257.0 6.4 %copy.8 = bf16[8192,256]{1,0:T(8,128)(2,1)} copy(bf16[8192,256]{0,1:T(8,128)(2,1)} %fusion.8) | data formatting | bytes 8388608 | tf_op jit(solution)/shard_map/jit(_roll_dynamic)/dynamic_slice | solution.py:19
  263.3 0.0 collective-permute-done.1
  263.3 7.9 %fusion.5 = bf16[8192,256]{0,1:T(8,128)(2,1)} fusion(s32[]{:T(128)S(6)} %select_n.22, bf16[8192,128]{0,1:T(8,128)(2,1)S(1)} %convolution_convert_fusion.1, bf16[8192,128]{0,1:T(8,128)(2,1)} %collective-permute-done.1), kind=kLoop, calls=%fused_computation.18 | loop fusion | flops 16777216 | bytes 8388612 | tf_op jit(solution)/shard_map/jit(_roll_dynamic)/concatenate | solution.py:19
  271.2 6.4 %copy.9 = bf16[8192,256]{1,0:T(8,128)(2,1)} copy(bf16[8192,256]{0,1:T(8,128)(2,1)} %fusion.5) | data formatting | bytes 8388608 | tf_op jit(solution)/shard_map/jit(_roll_dynamic)/dynamic_slice | solution.py:19
  (1 shorter events, 0.0 us)
Async XLA Ops:
  7.2 223.3 %copy-start = (bf16[2304,1,256]{2,0,1:T(8,128)(2,1)S(1)}, bf16[2304,1,256]{2,0,1:T(8,128)(2,1)}, u32[]{:S(2)}) copy-start(bf16[2304,1,256]{2,0,1:T(8,128)(2,1)} %param.9) | copy-start | bytes 3538948
  7.2 185.6 %copy-start.1 = (bf16[2304,128]{1,0:T(8,128)(2,1)S(1)}, bf16[2304,128]{1,0:T(8,128)(2,1)}, u32[]{:S(2)}) copy-start(bf16[2304,128]{1,0:T(8,128)(2,1)} %param.10) | copy-start | bytes 1769476
  7.2 185.5 %all-gather.2.cloned.1.call-start = ((), (), s32[]{:S(2)}) async-start(), calls=%async_computation | async-start | bytes 42467328 | tf_op jit(solution)/shard_map/all_gather | solution.py:25
  212.0 37.1 %collective-permute-start = (bf16[8192,128]{0,1:T(8,128)(2,1)}, bf16[8192,128]{0,1:T(8,128)(2,1)}, u32[]{:S(2)}, u32[]{:S(2)}) collective-permute-start(bf16[8192,128]{0,1:T(8,128)(2,1)} %convolution_convert_fusion.2), channel_id=1, source_target_pairs={{0,1},{1,0},{2,3},{3,2},{4,5},{5,4},{6,7},{7,6}} | collective-permute-start | bytes 6291464 | tf_op jit(solution)/shard_map/ppermute | solution.py:17
  230.2 33.2 %collective-permute-start.1 = (bf16[8192,128]{0,1:T(8,128)(2,1)S(1)}, bf16[8192,128]{0,1:T(8,128)(2,1)}, u32[]{:S(2)}, u32[]{:S(2)}) collective-permute-start(bf16[8192,128]{0,1:T(8,128)(2,1)S(1)} %convolution_convert_fusion.1), channel_id=1, source_target_pairs={{0,1},{1,0},{2,3},{3,2},{4,5},{5,4},{6,7},{7,6}} | collective-permute-start | bytes 6291464 | tf_op jit(solution)/shard_map/ppermute | solution.py:17
Sparse Core Ops, SparseCore 0:
  16.5 176.2 all-gather.1
where the time goes:
time: 285 us; the launch traced here: 284 us
  waiting for transfers between devices  176 us (62%)
  matrix products  55.8 us (20%)
  other arithmetic  24.9 us (9%)
  between operations  14.1 us (5%)
  local copies, waits for them, and re-layouts  12.7 us (4%)
    all_gather x1, waiting for transfers between devices, local_step(): gathered = lax.all_gather(normed, 'tp', axis=0, tiled=True)  176 us
    dot_general x1, matrix products, local_step(): jnp.dot(gathered, w_k, preferred_element_type=jnp.float32)  19.2 us
    dot_general x1, matrix products, local_step(): jnp.einsum('td,dhe->the', gathered, w_q, preferred_element_type=jnp.float32)  18.6 us
    dot_general x1, matrix products, local_step(): jnp.dot(gathered, w_v, preferred_element_type=jnp.float32)  17.9 us
    concatenate x2, other arithmetic, head_pieces(): return jnp.roll(joined, member * piece.shape[1], axis=1)  15.8 us
    dynamic_slice x2, local copies, waits for them, and re-layouts, head_pieces(): return jnp.roll(joined, member * piece.shape[1], axis=1)  12.7 us
  transfers between devices with their start and end apart: 3, of which 1 were waited for; matrix products, arithmetic and copies ran while one was open for 18% of the time, Pallas kernels for 0%

commit v1 on v0

v1 whole, which is shorter than its diff:
```python
import jax
import jax.numpy as jnp
from jax import lax
from jax.experimental import pallas as pl
from jax.experimental.pallas import tpu as pltpu
from jax.sharding import PartitionSpec as P

EPSILON = 1e-6
CHUNK = 256
PIECE = 16


def kernel(x_hbm, gain, wq_hbm, wk_hbm, wv_hbm, q_out, k_out, v_out,
           x_own, x_side, w_own, w_far, far_out, mate_q,
           load_x, load_w, mw_send, mw_recv, fw_send, fw_recv, rw_send, rw_recv,
           x_send, x_recv, m_send, m_recv, f_send, fq_recv, fkv_recv, r_send, r_recv):
    rows, width = x_hbm.shape
    head = wq_hbm.shape[1]
    part = wk_hbm.shape[1]
    chunks = rows // CHUNK

    me = lax.axis_index("tp")
    core = lax.rem(me, 2)
    mate = me + 1 - 2 * core
    side = me + 2 - 4 * lax.rem(me // 2, 2)
    far = me + 4 - 8 * (me // 4)
    far_mate = far + 1 - 2 * core
    far_chip = far - core

    barrier = pltpu.get_barrier_semaphore()
    for peer in (mate, side, far, far_mate):
        pl.semaphore_signal(barrier, inc=1, device_id={"tp": peer})

    def send(src, dst, send_sem, recv_sem, to):
        return pltpu.make_async_remote_copy(src_ref=src, dst_ref=dst, send_sem=send_sem, recv_sem=recv_sem, device_id={"tp": to})

    q_cols = pl.ds(pl.multiple_of(core * head, head), head)
    k_cols = pl.ds(pl.multiple_of(2 * head + core * part, part), part)
    v_cols = pl.ds(pl.multiple_of(3 * head + core * part, part), part)
    mine = ((wk_hbm, k_cols), (wv_hbm, v_cols), (wq_hbm, q_cols))

    local_w = [pltpu.make_async_copy(src, w_own.at[:, cols], load_w.at[i]) for i, (src, cols) in enumerate(mine)]
    mate_w = [send(src, w_own.at[:, cols], mw_send.at[i], mw_recv.at[i], mate) for i, (src, cols) in enumerate(mine)]
    far_w = [send(src, w_far.at[:, cols], fw_send.at[i], fw_recv.at[i], far) for i, (src, cols) in enumerate(mine)]
    relay_w = [send(w_far.at[:, cols], w_far.at[:, cols], rw_send.at[i], rw_recv.at[i], mate) for i, (src, cols) in enumerate(mine)]

    def chunk_rows(i):
        return pl.ds(pl.multiple_of(i * CHUNK, CHUNK), CHUNK)

    def load_chunk(i):
        return pltpu.make_async_copy(x_hbm.at[chunk_rows(i), :], x_own.at[chunk_rows(i), :], load_x.at[i])

    def side_chunk(i):
        return send(x_hbm.at[chunk_rows(i), :], x_side.at[chunk_rows(i), :], x_send.at[i], x_recv.at[i], side)

    for i in range(chunks):
        load_chunk(i).start()
    for copy in local_w:
        copy.start()

    pl.semaphore_wait(barrier, 4)
    for i in range(3):
        far_w[i].start()
    side_chunk(0).start()
    for i in range(3):
        mate_w[i].start()
    for i in range(1, chunks):
        side_chunk(i).start()

    def normalise(ref, i):
        def piece(p, carry):
            at = pl.ds(pl.multiple_of(i * CHUNK + p * PIECE, PIECE), PIECE)
            x_wide = ref[at, :].astype(jnp.float32)
            mean_sq = jnp.mean(x_wide * x_wide, axis=-1, keepdims=True)
            ref[at, :] = (x_wide * lax.rsqrt(mean_sq + EPSILON) * gain[...]).astype(jnp.bfloat16)
            return carry

        lax.fori_loop(0, CHUNK // PIECE, piece, 0, unroll=2)

    def product(ref, i, w, start):
        return jnp.dot(ref[chunk_rows(i), :], w[:, start], preferred_element_type=jnp.float32).astype(jnp.bfloat16)

    def columns(block):
        if isinstance(block, int):
            return slice(block * head, (block + 1) * head)
        return pl.ds(pl.multiple_of(block * head, head), head)

    def out_rows(device, i):
        return pl.ds(pl.multiple_of(device * rows + i * CHUNK, CHUNK), CHUNK)

    def source(device, n):
        across = device + 2 - 4 * lax.rem(device // 2, 2)
        return jnp.where(n < chunks, device, across), lax.rem(n, chunks)

    def slot_rows(device, n):
        return out_rows(*source(device, n))

    def stage_rows(n):
        return pl.ds(pl.multiple_of(n * CHUNK, CHUNK), CHUNK)

    def mate_copies(n):
        at = slot_rows(me, n)
        return [
            send(k_out.at[at, :], k_out.at[at, :], m_send.at[0, n], m_recv.at[0, n], mate),
            send(v_out.at[at, :], v_out.at[at, :], m_send.at[1, n], m_recv.at[1, n], mate),
            send(mate_q.at[stage_rows(n), :], q_out.at[at, :], m_send.at[2, n], m_recv.at[2, n], mate),
        ]

    def far_kv(n):
        at = slot_rows(me, n)
        return [
            send(far_out.at[2, stage_rows(n), :], k_out.at[at, :], f_send.at[2, n], fkv_recv.at[0, n], far),
            send(far_out.at[3, stage_rows(n), :], v_out.at[at, :], f_send.at[3, n], fkv_recv.at[1, n], far),
        ]

    def far_q(n):
        at = slot_rows(me, n)
        return [
            send(far_out.at[j, stage_rows(n), :], q_out.at[at, :], f_send.at[j, n], fq_recv.at[core, n], far_chip + j)
            for j in range(2)
        ]

    def relay_copies(n):
        at = slot_rows(far, n)
        return [
            send(ref.at[at, :], ref.at[at, :], r_send.at[j, n], r_recv.at[j, n], mate)
            for j, ref in enumerate((k_out, v_out))
        ]

    def near_products(ref, i, n):
        at = slot_rows(me, n)
        k_out[at, :] = product(ref, i, w_own, columns(2))
        v_out[at, :] = product(ref, i, w_own, columns(3))
        q_out[at, :] = product(ref, i, w_own, columns(core))
        mate_q[stage_rows(n), :] = product(ref, i, w_own, columns(1 - core))
        for copy in mate_copies(n):
            copy.start()

    def far_kv_products(ref, i, n):
        for block in (2, 3):
            far_out[block, stage_rows(n), :] = product(ref, i, w_far, columns(block))
        for copy in far_kv(n):
            copy.start()

    def far_q_products(ref, i, n):
        for block in (0, 1):
            far_out[block, stage_rows(n), :] = product(ref, i, w_far, columns(block))
        for copy in far_q(n):
            copy.start()

    def loop(count, body):
        def step(i, carry):
            body(i)
            return carry

        lax.fori_loop(0, count, step, 0)

    def own_norm(i):
        load_chunk(i).wait()
        normalise(x_own, i)

    loop(chunks, own_norm)
    for i in range(3):
        local_w[i].wait()
        mate_w[i].wait_recv()
    loop(chunks, lambda i: near_products(x_own, i, i))

    for i in (0, 1):
        far_w[i].wait_recv()
        relay_w[i].start()
    for i in (0, 1):
        relay_w[i].wait_recv()
    loop(chunks, lambda i: far_kv_products(x_own, i, i))
    far_w[2].wait_recv()
    relay_w[2].start()
    relay_w[2].wait_recv()
    loop(chunks, lambda i: far_q_products(x_own, i, i))

    def side_step(i):
        side_chunk(i).wait_recv()
        normalise(x_side, i)
        far_kv_products(x_side, i, chunks + i)
        far_q_products(x_side, i, chunks + i)
        near_products(x_side, i, chunks + i)

    loop(chunks, side_step)

    def relay_step(n):
        for arrived, onward in zip(far_kv(n), relay_copies(n)):
            arrived.wait_recv()
            onward.start()

    loop(2 * chunks, relay_step)

    def drain(n):
        for copy in mate_copies(n):
            copy.wait_send()
            copy.wait_recv()
        for copy in far_kv(n):
            copy.wait_send()
        for j, copy in enumerate(far_q(n)):
            copy.wait_send()
            pltpu.make_async_remote_copy(
                src_ref=far_out.at[j, stage_rows(n), :], dst_ref=q_out.at[slot_rows(me, n), :], send_sem=f_send.at[j, n],
                recv_sem=fq_recv.at[j, n], device_id={"tp": far},
            ).wait_recv()
        for copy in relay_copies(n):
            copy.wait_send()
            copy.wait_recv()

    loop(2 * chunks, drain)
    for copies in (mate_w, far_w, relay_w):
        for copy in copies:
            copy.wait_send()
    loop(chunks, lambda i: side_chunk(i).wait_send())


def solution(mesh):
    group_size = mesh.shape["tp"]

    def local_step(x_rows, norm_gain, w_q, w_k, w_v):
        rows, width = x_rows.shape
        head = w_q.shape[2]
        slots = 2 * (rows // CHUNK)
        chunks = rows // CHUNK
        dma = pltpu.SemaphoreType.DMA
        any_space = pl.BlockSpec(memory_space=pl.ANY)
        vmem = pl.BlockSpec(memory_space=pltpu.VMEM)
        outs = pl.pallas_call(
            kernel,
            out_shape=[pltpu.VMEM((group_size * rows, head), jnp.bfloat16)] * 3,
            in_specs=[any_space, vmem, any_space, any_space, any_space],
            out_specs=[vmem] * 3,
            scratch_shapes=[
                pltpu.VMEM((rows, width), jnp.bfloat16),
                pltpu.VMEM((rows, width), jnp.bfloat16),
                pltpu.VMEM((width, 4 * head), jnp.bfloat16),
                pltpu.VMEM((width, 4 * head), jnp.bfloat16),
                pltpu.VMEM((4, 2 * rows, head), jnp.bfloat16),
                pltpu.VMEM((2 * rows, head), jnp.bfloat16),
                dma((chunks,)), dma((3,)), dma((3,)), dma((3,)), dma((3,)), dma((3,)), dma((3,)), dma((3,)),
                dma((chunks,)), dma((chunks,)), dma((3, slots)), dma((3, slots)), dma((4, slots)), dma((2, slots)),
                dma((2, slots)), dma((2, slots)), dma((2, slots)),
            ],
            compiler_params=pltpu.CompilerParams(collective_id=0, has_side_effects=True, vmem_limit_bytes=44 * 1024 * 1024),
        )(x_rows, norm_gain.reshape(1, width), w_q.reshape(width, head), w_k, w_v)
        return tuple(out[:, None, :] for out in outs)

    return jax.shard_map(local_step, mesh=mesh, in_specs=(P(("dp", "tp"), None), P(None), P(None, "tp", None), P(None, "tp"), P(None, "tp")), out_specs=(P("dp", "tp", None), P("dp", "tp", None), P("dp", "tp", None)), check_vma=False)
```

time: 285 us -> 155 us (0.54)
  waiting for transfers between devices: 176 us -> 0 us
  Pallas kernels: 0 us -> 147 us
  matrix products: 55.8 us -> 0 us
  other arithmetic: 24.9 us -> 0 us
  between operations: 14.1 us -> 0.64 us
  local copies, waits for them, and re-layouts: 12.7 us -> 7.35 us
    all_gather x1 -> x0, waiting for transfers between devices: 176 us -> none  [local_step(): gathered = lax.all_gather(normed, 'tp', axis=0, tiled=True)]
    pallas_call x0 -> x1, Pallas kernels: none -> 147 us  [local_step(): pl.pallas_call(kernel, out_shape=[pltpu.VMEM((group_size * rows, head), j...]
    dot_general x3 -> x0, matrix products: 55.8 us -> none  [the longest x1 19.2 us: local_step(): jnp.dot(gathered, w_k, preferred_element_type=jnp.float32)]
    concatenate x2 -> x0, other arithmetic: 15.8 us -> none  [head_pieces(): return jnp.roll(joined, member * piece.shape[1], axis=1)]
    dynamic_slice x2 -> x0, local copies, waits for them, and re-layouts: 12.7 us -> none  [head_pieces(): return jnp.roll(joined, member * piece.shape[1], axis=1)]
    unnamed x4 -> x3, local copies, waits for them, and re-layouts: 0.01 us -> 6.04 us
    convert_element_type x1 -> x0, other arithmetic: 5.63 us -> none  [local_step(): (x_wide * lax.rsqrt(mean_sq + EPSILON) * norm_gain).astype(jnp.bfloat16)]
    reduce_sum x1 -> x0, other arithmetic: 3.46 us -> none  [local_step(): mean_sq = jnp.mean(x_wide * x_wide, axis=-1, keepdims=True)]
  transfers between devices with their start and end apart: 3 -> 0, of which waited for: 1 -> 0; matrix products, arithmetic and copies ran while one was open for 18% -> 0% of each run, Pallas kernels for 0% -> 0%
where the time goes in v1:
time: 155 us
  Pallas kernels  147 us (95%)
  local copies, waits for them, and re-layouts  7.35 us (5%)
    pallas_call x1, Pallas kernels, local_step(): pl.pallas_call(kernel, out_shape=[pltpu.VMEM((group_size * rows, head), j...  147 us
    unnamed x3, local copies, waits for them, and re-layouts  6.04 us

profile of v1, /device:TPU:1, one launch (start us, length us, event | category | flops | bytes accessed | tf_op | source)
XLA Modules:
  0.0 155.0 jit_solution(7619641527617428499)
XLA Ops:
  0.6 1.3 reshape.12.gain
  1.9 147.0 %shard_map.76 = (bf16[8192,256]{1,0:T(8,128)(2,1)S(1)}, bf16[8192,256]{1,0:T(8,128)(2,1)S(1)}, bf16[8192,256]{1,0:T(8,128)(2,1)S(1)}) custom-call(bf16[1024,2304]{1,0:T(8,128)(2,1)} %x_hbm.1, f32[1,2304]{1,0:T(1,128)} %reshape.12.gain, bf16[2304,256]{1,0:T(8,128)(2,1)} %bitcast.7, bf16[2304,128]{1,0:T(8,128)(2,1)} %wk_hbm.1, bf16[2304,128]{1,0:T(8,128)(2,1)} %wv_hbm.1), custom_call_target="tpu_custom_call" | custom-call | tf_op jit(solution)/shard_map/pallas_call | solution.py:229
  148.9 2.0 %copy.11 = bf16[8192,1,256]{2,0,1:T(8,128)(2,1)} copy(bf16[8192,1,256]{2,0,1:T(8,128)(2,1)S(1)} %bitcast.6) | data formatting | bytes 8388608
  151.0 2.0 %copy.12 = bf16[8192,1,256]{2,0,1:T(8,128)(2,1)} copy(bf16[8192,1,256]{2,0,1:T(8,128)(2,1)S(1)} %bitcast.5) | data formatting | bytes 8388608
  153.0 2.0 %copy.13 = bf16[8192,1,256]{2,0,1:T(8,128)(2,1)} copy(bf16[8192,1,256]{2,0,1:T(8,128)(2,1)S(1)} %bitcast.4) | data formatting | bytes 8388608

commit v2 on v1

--- a/solution.py
+++ b/solution.py
@@ -8,11 +8,12 @@
 EPSILON = 1e-6
 CHUNK = 256
 PIECE = 16
-
-
-def kernel(x_hbm, gain, wq_hbm, wk_hbm, wv_hbm, q_out, k_out, v_out,
-           x_own, x_side, w_own, w_far, far_out, mate_q,
-           load_x, load_w, mw_send, mw_recv, fw_send, fw_recv, rw_send, rw_recv,
+STORES = 4
+
+
+def kernel(x_hbm, gain_hbm, wq_hbm, wk_hbm, wv_hbm, q_out, k_out, v_out,
+           x_own, x_side, w_own, w_far, far_out, mate_q, gain,
+           load_gain, load_x, load_w, mw_send, mw_recv, fw_send, fw_recv, rw_send, rw_recv,
            x_send, x_recv, m_send, m_recv, f_send, fq_recv, fkv_recv, r_send, r_recv):
     rows, width = x_hbm.shape
     head = wq_hbm.shape[1]
@@ -53,6 +54,8 @@
     def side_chunk(i):
         return send(x_hbm.at[chunk_rows(i), :], x_side.at[chunk_rows(i), :], x_send.at[i], x_recv.at[i], side)
 
+    gain_copy = pltpu.make_async_copy(gain_hbm, gain, load_gain)
+    gain_copy.start()
     for i in range(chunks):
         load_chunk(i).start()
     for copy in local_w:
@@ -72,7 +75,7 @@
             at = pl.ds(pl.multiple_of(i * CHUNK + p * PIECE, PIECE), PIECE)
             x_wide = ref[at, :].astype(jnp.float32)
             mean_sq = jnp.mean(x_wide * x_wide, axis=-1, keepdims=True)
-            ref[at, :] = (x_wide * lax.rsqrt(mean_sq + EPSILON) * gain[...]).astype(jnp.bfloat16)
+            ref[at, :] = (x_wide * lax.rsqrt(mean_sq + EPSILON) * gain[...].reshape(1, width)).astype(jnp.bfloat16)
             return carry
 
         lax.fori_loop(0, CHUNK // PIECE, piece, 0, unroll=2)
@@ -159,6 +162,7 @@
         load_chunk(i).wait()
         normalise(x_own, i)
 
+    gain_copy.wait()
     loop(chunks, own_norm)
     for i in range(3):
         local_w[i].wait()
@@ -185,34 +189,50 @@
 
     loop(chunks, side_step)
 
+    def drain(n):
+        for copy in mate_copies(n):
+            copy.wait_send()
+            copy.wait_recv()
+        for copy in relay_copies(n):
+            copy.wait_send()
+            copy.wait_recv()
+        for copy in far_kv(n):
+            copy.wait_send()
+        for j, copy in enumerate(far_q(n)):
+            copy.wait_send()
+            send(far_out.at[j, stage_rows(n), :], q_out.at[slot_rows(me, n), :], f_send.at[j, n], fq_recv.at[j, n], far).wait_recv()
+
+    for copies in (mate_w, far_w, relay_w):
+        for copy in copies:
+            copy.wait_send()
+    loop(chunks, lambda i: side_chunk(i).wait_send())
+
     def relay_step(n):
         for arrived, onward in zip(far_kv(n), relay_copies(n)):
             arrived.wait_recv()
             onward.start()
 
+        @pl.when(n > 0)
+        def _():
+            drain(n - 1)
+
     loop(2 * chunks, relay_step)
-
-    def drain(n):
-        for copy in mate_copies(n):
-            copy.wait_send()
-            copy.wait_recv()
-        for copy in far_kv(n):
-            copy.wait_send()
-        for j, copy in enumerate(far_q(n)):
-            copy.wait_send()
-            pltpu.make_async_remote_copy(
-                src_ref=far_out.at[j, stage_rows(n), :], dst_ref=q_out.at[slot_rows(me, n), :], send_sem=f_send.at[j, n],
-                recv_sem=fq_recv.at[j, n], device_id={"tp": far},
-            ).wait_recv()
-        for copy in relay_copies(n):
-            copy.wait_send()
-            copy.wait_recv()
-
-    loop(2 * chunks, drain)
-    for copies in (mate_w, far_w, relay_w):
-        for copy in copies:
-            copy.wait_send()
-    loop(chunks, lambda i: side_chunk(i).wait_send())
+    drain(2 * chunks - 1)
+
+
+def store(*refs):
+    count = len(refs) // 2
+    sources, targets, sems = refs[:count], refs[count:2 * count], refs[2 * count]
+    size = sources[0].shape[0] // STORES
+    copies = [
+        pltpu.make_async_copy(source.at[pl.ds(i * size, size), :], target.at[pl.ds(i * size, size), :], sems.at[o, i])
+        for o, (source, target) in enumerate(zip(sources, targets))
+        for i in range(STORES)
+    ]
+    for copy in copies:
+        copy.start()
+    for copy in copies:
+        copy.wait()
 
 
 def solution(mesh):
@@ -229,7 +249,7 @@
         outs = pl.pallas_call(
             kernel,
             out_shape=[pltpu.VMEM((group_size * rows, head), jnp.bfloat16)] * 3,
-            in_specs=[any_space, vmem, any_space, any_space, any_space],
+            in_specs=[any_space] * 5,
             out_specs=[vmem] * 3,
             scratch_shapes=[
                 pltpu.VMEM((rows, width), jnp.bfloat16),
@@ -238,12 +258,21 @@
                 pltpu.VMEM((width, 4 * head), jnp.bfloat16),
                 pltpu.VMEM((4, 2 * rows, head), jnp.bfloat16),
                 pltpu.VMEM((2 * rows, head), jnp.bfloat16),
-                dma((chunks,)), dma((3,)), dma((3,)), dma((3,)), dma((3,)), dma((3,)), dma((3,)), dma((3,)),
+                pltpu.VMEM((width,), jnp.float32),
+                dma(()), dma((chunks,)), dma((3,)), dma((3,)), dma((3,)), dma((3,)), dma((3,)), dma((3,)), dma((3,)),
                 dma((chunks,)), dma((chunks,)), dma((3, slots)), dma((3, slots)), dma((4, slots)), dma((2, slots)),
                 dma((2, slots)), dma((2, slots)), dma((2, slots)),
             ],
             compiler_params=pltpu.CompilerParams(collective_id=0, has_side_effects=True, vmem_limit_bytes=44 * 1024 * 1024),
-        )(x_rows, norm_gain.reshape(1, width), w_q.reshape(width, head), w_k, w_v)
+        )(x_rows, norm_gain, w_q.reshape(width, head), w_k, w_v)
+        outs = pl.pallas_call(
+            store,
+            out_shape=[pltpu.HBM((group_size * rows, head), jnp.bfloat16)] * 3,
+            in_specs=[vmem] * 3,
+            out_specs=[pl.BlockSpec(memory_space=pltpu.HBM)] * 3,
+            scratch_shapes=[dma((3, STORES))],
+            compiler_params=pltpu.CompilerParams(vmem_limit_bytes=1024 * 1024),
+        )(*(pltpu.with_memory_space_constraint(out, pltpu.VMEM) for out in outs))
         return tuple(out[:, None, :] for out in outs)
 
     return jax.shard_map(local_step, mesh=mesh, in_specs=(P(("dp", "tp"), None), P(None), P(None, "tp", None), P(None, "tp"), P(None, "tp")), out_specs=(P("dp", "tp", None), P("dp", "tp", None), P("dp", "tp", None)), check_vma=False)

time: 155 us -> 152 us (0.981)
  local copies, waits for them, and re-layouts: 7.35 us -> 0 us
  Pallas kernels: 147 us -> 151 us
    unnamed x3 -> x0, local copies, waits for them, and re-layouts: 6.04 us -> none
    pallas_call x0 -> x1, Pallas kernels: none -> 4.67 us  [local_step(): pl.pallas_call(store, out_shape=[pltpu.HBM((group_size * rows, head), jnp...]
where the time goes in v2:
time: 152 us
  Pallas kernels  151 us (99%)
    pallas_call x1, Pallas kernels, local_step(): pl.pallas_call(kernel, out_shape=[pltpu.VMEM((group_size * rows, head), j...  146 us
    pallas_call x1, Pallas kernels, local_step(): pl.pallas_call(store, out_shape=[pltpu.HBM((group_size * rows, head), jnp...  4.67 us

profile of v2, /device:TPU:1, one launch (start us, length us, event | category | flops | bytes accessed | tf_op | source)
XLA Modules:
  0.0 151.6 jit_solution(11011507677517696213)
XLA Ops:
  0.6 146.3 %shard_map.76 = (bf16[8192,256]{1,0:T(8,128)(2,1)S(1)}, bf16[8192,256]{1,0:T(8,128)(2,1)S(1)}, bf16[8192,256]{1,0:T(8,128)(2,1)S(1)}) custom-call(bf16[1024,2304]{1,0:T(8,128)(2,1)} %x_hbm.1, f32[2304]{0:T(1024)} %gain_hbm.1, bf16[2304,256]{1,0:T(8,128)(2,1)} %bitcast.4, bf16[2304,128]{1,0:T(8,128)(2,1)} %wk_hbm.1, bf16[2304,128]{1,0:T(8,128)(2,1)} %wv_hbm.1), custom_call_target="tpu_custom_call" | custom-call | tf_op jit(solution)/shard_map/pallas_call | solution.py:249
  146.9 4.7 %shard_map.77 = (bf16[8192,256]{1,0:T(8,128)(2,1)}, bf16[8192,256]{1,0:T(8,128)(2,1)}, bf16[8192,256]{1,0:T(8,128)(2,1)}) custom-call(bf16[8192,256]{1,0:T(8,128)(2,1)S(1)} %get-tuple-element.9.refs_0_, bf16[8192,256]{1,0:T(8,128)(2,1)S(1)} %get-tuple-element.10.refs_1_, bf16[8192,256]{1,0:T(8,128)(2,1)S(1)} %get-tuple-element.11.refs_2_), custom_call_target="tpu_custom_call" | custom-call | tf_op jit(solution)/shard_map/pallas_call | solution.py:268

commit v3 on v2

--- a/solution.py
+++ b/solution.py
@@ -13,7 +13,7 @@
 
 def kernel(x_hbm, gain_hbm, wq_hbm, wk_hbm, wv_hbm, q_out, k_out, v_out,
            x_own, x_side, w_own, w_far, far_out, mate_q, gain,
-           load_gain, load_x, load_w, mw_send, mw_recv, fw_send, fw_recv, rw_send, rw_recv,
+           answer, load_gain, load_x, load_w, mw_send, mw_recv, fw_send, fw_recv, rw_send, rw_recv,
            x_send, x_recv, m_send, m_recv, f_send, fq_recv, fkv_recv, r_send, r_recv):
     rows, width = x_hbm.shape
     head = wq_hbm.shape[1]
@@ -23,14 +23,19 @@
     me = lax.axis_index("tp")
     core = lax.rem(me, 2)
     mate = me + 1 - 2 * core
-    side = me + 2 - 4 * lax.rem(me // 2, 2)
-    far = me + 4 - 8 * (me // 4)
+    row = me // 4
+    side = me + 4 - 8 * row
+    far = me + 2 - 4 * lax.rem(me // 2, 2)
     far_mate = far + 1 - 2 * core
     far_chip = far - core
 
     barrier = pltpu.get_barrier_semaphore()
-    for peer in (mate, side, far, far_mate):
+    for peer in (mate, far, far_mate):
         pl.semaphore_signal(barrier, inc=1, device_id={"tp": peer})
+
+    @pl.when(row == 0)
+    def _():
+        pl.semaphore_signal(barrier, inc=1, device_id={"tp": side})
 
     def send(src, dst, send_sem, recv_sem, to):
         return pltpu.make_async_remote_copy(src_ref=src, dst_ref=dst, send_sem=send_sem, recv_sem=recv_sem, device_id={"tp": to})
@@ -61,13 +66,22 @@
     for copy in local_w:
         copy.start()
 
-    pl.semaphore_wait(barrier, 4)
+    pl.semaphore_wait(barrier, 3 + row)
     for i in range(3):
         far_w[i].start()
-    side_chunk(0).start()
+
+    @pl.when(row == 1)
+    def _():
+        pl.semaphore_signal(answer, inc=1, device_id={"tp": side})
+
     for i in range(3):
         mate_w[i].start()
-    for i in range(1, chunks):
+
+    @pl.when(row == 0)
+    def _():
+        pl.semaphore_wait(answer, 1)
+
+    for i in range(chunks):
         side_chunk(i).start()
 
     def normalise(ref, i):
@@ -92,7 +106,7 @@
         return pl.ds(pl.multiple_of(device * rows + i * CHUNK, CHUNK), CHUNK)
 
     def source(device, n):
-        across = device + 2 - 4 * lax.rem(device // 2, 2)
+        across = device + 4 - 8 * (device // 4)
         return jnp.where(n < chunks, device, across), lax.rem(n, chunks)
 
     def slot_rows(device, n):
@@ -259,7 +273,7 @@
                 pltpu.VMEM((4, 2 * rows, head), jnp.bfloat16),
                 pltpu.VMEM((2 * rows, head), jnp.bfloat16),
                 pltpu.VMEM((width,), jnp.float32),
-                dma(()), dma((chunks,)), dma((3,)), dma((3,)), dma((3,)), dma((3,)), dma((3,)), dma((3,)), dma((3,)),
+                pltpu.SemaphoreType.REGULAR, dma(()), dma((chunks,)), dma((3,)), dma((3,)), dma((3,)), dma((3,)), dma((3,)), dma((3,)), dma((3,)),
                 dma((chunks,)), dma((chunks,)), dma((3, slots)), dma((3, slots)), dma((4, slots)), dma((2, slots)),
                 dma((2, slots)), dma((2, slots)), dma((2, slots)),
             ],

time: 152 us -> 151 us (level)
  no operation moved by 1% of the time
where the time goes in v3:
time: 151 us
  Pallas kernels  150 us (99%)
    pallas_call x1, Pallas kernels, local_step(): pl.pallas_call(kernel, out_shape=[pltpu.VMEM((group_size * rows, head), j...  146 us
    pallas_call x1, Pallas kernels, local_step(): pl.pallas_call(store, out_shape=[pltpu.HBM((group_size * rows, head), jnp...  4.67 us

profile of v3, /device:TPU:1, one launch (start us, length us, event | category | flops | bytes accessed | tf_op | source)
XLA Modules:
  0.0 151.0 jit_solution(16236697132446552301)
XLA Ops:
  0.6 145.7 %shard_map.76 = (bf16[8192,256]{1,0:T(8,128)(2,1)S(1)}, bf16[8192,256]{1,0:T(8,128)(2,1)S(1)}, bf16[8192,256]{1,0:T(8,128)(2,1)S(1)}) custom-call(bf16[1024,2304]{1,0:T(8,128)(2,1)} %x_hbm.1, f32[2304]{0:T(1024)} %gain_hbm.1, bf16[2304,256]{1,0:T(8,128)(2,1)} %bitcast.4, bf16[2304,128]{1,0:T(8,128)(2,1)} %wk_hbm.1, bf16[2304,128]{1,0:T(8,128)(2,1)} %wv_hbm.1), custom_call_target="tpu_custom_call" | custom-call | tf_op jit(solution)/shard_map/pallas_call | solution.py:263
  146.4 4.7 %shard_map.77 = (bf16[8192,256]{1,0:T(8,128)(2,1)}, bf16[8192,256]{1,0:T(8,128)(2,1)}, bf16[8192,256]{1,0:T(8,128)(2,1)}) custom-call(bf16[8192,256]{1,0:T(8,128)(2,1)S(1)} %get-tuple-element.9.refs_0_, bf16[8192,256]{1,0:T(8,128)(2,1)S(1)} %get-tuple-element.10.refs_1_, bf16[8192,256]{1,0:T(8,128)(2,1)S(1)} %get-tuple-element.11.refs_2_), custom_call_target="tpu_custom_call" | custom-call | tf_op jit(solution)/shard_map/pallas_call | solution.py:282

commit v4 on v0

v4 whole, which is shorter than its diff:
```python
import functools

import jax
import jax.numpy as jnp
from jax import lax
from jax.experimental import pallas as pl
from jax.experimental.pallas import tpu as pltpu
from jax.sharding import PartitionSpec as P

EPSILON = 1e-6
CHUNK = 256
PIECE = 16

OWN, SIDE, MATE, MATE_SIDE, FAR, FAR_MATE = range(6)
LATE_FAR, LATE_FAR_MATE = range(2)
K, V, Q_SAME, Q_OTHER = range(4)


class Place:
    def __init__(self):
        self.me = lax.axis_index("tp")
        self.core = lax.rem(self.me, 2)
        self.row = self.me // 4
        self.mate = self.me + 1 - 2 * self.core
        self.side = self.across(self.me)
        self.far = self.me + 2 - 4 * lax.rem(self.me // 2, 2)
        self.far_mate = self.far + 1 - 2 * self.core
        self.first = 1 + 2 * self.core
        self.first_other = 3 - 2 * self.core

    def across(self, device):
        return device + 4 - 8 * (device // 4)


def send(src, dst, send_sem, recv_sem, to):
    return pltpu.make_async_remote_copy(src_ref=src, dst_ref=dst, send_sem=send_sem, recv_sem=recv_sem, device_id={"tp": to})


def signal(sem, to):
    pl.semaphore_signal(sem, inc=1, device_id={"tp": to})


def loop(start, stop, body):
    def step(i, carry):
        body(i)
        return carry

    lax.fori_loop(start, stop, step, 0)


def chunk_rows(i, base=0):
    return pl.ds(pl.multiple_of(base + i * CHUNK, CHUNK), CHUNK)


def gather(x_hbm, gain_hbm, wq_hbm, wk_hbm, wv_hbm, q_early, k_early, v_early, q_late, k_late, v_late, far_late,
           x_own, x_side, w_own, w_far, far_own, mate_q, gain,
           answer, load_gain, load_x, load_w, mw_send, mw_recv, fw_send, fw_recv, rw_send, rw_recv,
           x_send, x_recv, m_send, m_recv, f_send, f_recv, r_send, r_recv):
    rows, width = x_hbm.shape
    head = wq_hbm.shape[1]
    part = wk_hbm.shape[1]
    chunks = rows // CHUNK
    at = Place()
    core = at.core

    barrier = pltpu.get_barrier_semaphore()
    for peer in (at.mate, at.far, at.far_mate):
        signal(barrier, peer)

    @pl.when(at.row == 0)
    def _():
        signal(barrier, at.side)

    q_cols = pl.ds(pl.multiple_of(core * head, head), head)
    k_cols = pl.ds(pl.multiple_of(2 * head + core * part, part), part)
    v_cols = pl.ds(pl.multiple_of(3 * head + core * part, part), part)
    mine = ((wk_hbm, k_cols), (wv_hbm, v_cols), (wq_hbm, q_cols))
    local_w = [pltpu.make_async_copy(src, w_own.at[:, cols], load_w.at[i]) for i, (src, cols) in enumerate(mine)]
    mate_w = [send(w_own.at[:, cols], w_own.at[:, cols], mw_send.at[i], mw_recv.at[i], at.mate) for i, (src, cols) in enumerate(mine)]
    far_w = [send(w_own.at[:, cols], w_far.at[:, cols], fw_send.at[i], fw_recv.at[i], at.far) for i, (src, cols) in enumerate(mine)]
    relay_w = [send(w_far.at[:, cols], w_far.at[:, cols], rw_send.at[i], rw_recv.at[i], at.mate) for i, (src, cols) in enumerate(mine)]

    def load_chunk(i):
        return pltpu.make_async_copy(x_hbm.at[chunk_rows(i), :], x_own.at[chunk_rows(i), :], load_x.at[i])

    def side_chunk(i):
        return send(x_hbm.at[chunk_rows(i), :], x_side.at[chunk_rows(i), :], x_send.at[i], x_recv.at[i], at.side)

    for copy in local_w:
        copy.start()
    gain_copy = pltpu.make_async_copy(gain_hbm, gain, load_gain)
    gain_copy.start()
    for i in range(chunks):
        load_chunk(i).start()

    pl.semaphore_wait(barrier, 3 + at.row)
    for i in range(3):
        local_w[i].wait()
        far_w[i].start()

    @pl.when(at.row == 1)
    def _():
        signal(answer, at.side)

    for copy in mate_w:
        copy.start()

    @pl.when(at.row == 0)
    def _():
        pl.semaphore_wait(answer, 1)

    for i in range(chunks):
        side_chunk(i).start()

    def normalise(ref, i):
        def piece(p, carry):
            here = pl.ds(pl.multiple_of(i * CHUNK + p * PIECE, PIECE), PIECE)
            x_wide = ref[here, :].astype(jnp.float32)
            mean_sq = jnp.mean(x_wide * x_wide, axis=-1, keepdims=True)
            ref[here, :] = (x_wide * lax.rsqrt(mean_sq + EPSILON) * gain[...].reshape(1, width)).astype(jnp.bfloat16)
            return carry

        lax.fori_loop(0, CHUNK // PIECE, piece, 0, unroll=2)

    def product(ref, i, w, block):
        cols = slice(block * head, (block + 1) * head) if isinstance(block, int) else pl.ds(pl.multiple_of(block * head, head), head)
        return jnp.dot(ref[chunk_rows(i), :], w[:, cols], preferred_element_type=jnp.float32).astype(jnp.bfloat16)

    far_columns = {K: 2, V: 3, Q_SAME: core, Q_OTHER: 1 - core}

    def mate_copies(block, i):
        n = block * chunks + i
        here, there = chunk_rows(i, block * rows), chunk_rows(i, (MATE + block) * rows)
        sources = (k_early.at[here, :], v_early.at[here, :], mate_q.at[here, :])
        return [send(src, dst.at[there, :], m_send.at[j, n], m_recv.at[j, n], at.mate)
                for j, (src, dst) in enumerate(zip(sources, (k_early, v_early, q_early)))]

    def near_products(ref, block, i):
        here = chunk_rows(i, block * rows)
        k_early[here, :] = product(ref, i, w_own, 2)
        v_early[here, :] = product(ref, i, w_own, 3)
        q_early[here, :] = product(ref, i, w_own, core)
        mate_q[here, :] = product(ref, i, w_own, 1 - core)
        for copy in mate_copies(block, i):
            copy.start()

    def far_products(ref, stage, kinds, i):
        for kind in kinds:
            stage[kind, chunk_rows(i), :] = product(ref, i, w_far, far_columns[kind])

    def own_message(kind, i):
        dst = {K: k_early, V: v_early, Q_SAME: q_early, Q_OTHER: q_early}[kind]
        there = chunk_rows(i, (FAR_MATE if kind == Q_OTHER else FAR) * rows)
        return send(far_own.at[kind, chunk_rows(i), :], dst.at[there, :], f_send.at[kind, i], f_recv.at[kind, i],
                    at.far_mate if kind == Q_OTHER else at.far)

    side_message = functools.partial(late_message, at, rows, chunks, far_late, (k_late, v_late, q_late, q_late), f_send, f_recv)

    def relay(j, i):
        ref = (k_early, v_early)[j]
        return send(ref.at[chunk_rows(i, FAR * rows), :], ref.at[chunk_rows(i, FAR_MATE * rows), :], r_send.at[j, i], r_recv.at[j, i], at.mate)

    def own_norm(i):
        load_chunk(i).wait()
        normalise(x_own, i)

    gain_copy.wait()
    loop(0, chunks, own_norm)
    for copy in mate_w:
        copy.wait_recv()
    loop(0, chunks, lambda i: near_products(x_own, OWN, i))

    def far_step(kinds, i):
        far_products(x_own, far_own, kinds, i)
        for kind in kinds:
            own_message(kind, i).start()

    for i in (0, 1):
        far_w[i].wait_recv()
        relay_w[i].start()
    for i in (0, 1):
        relay_w[i].wait_recv()
    loop(0, chunks, functools.partial(far_step, (K, V)))
    far_w[2].wait_recv()
    relay_w[2].start()
    relay_w[2].wait_recv()
    loop(0, chunks, functools.partial(far_step, (Q_SAME, Q_OTHER)))

    def side_step(i):
        side_chunk(i).wait_recv()
        normalise(x_side, i)
        far_products(x_side, far_late, (Q_OTHER, K, V, Q_SAME), i)

        @pl.when(i < at.first)
        def _():
            side_message(Q_OTHER, i).start()

        @pl.when(i == at.first - 1)
        def _():
            loop(0, at.first, start_same)

        near_products(x_side, SIDE, i)

    def start_same(i):
        for kind in (K, V, Q_SAME):
            side_message(kind, i).start()

    loop(0, chunks, side_step)

    def relay_step(i):
        for j, kind in enumerate((K, V)):
            own_message(kind, i).wait_recv()
            relay(j, i).start()

    loop(0, chunks, relay_step)

    for copies in (mate_w, far_w, relay_w):
        for copy in copies:
            copy.wait_send()

    def drain(i):
        side_chunk(i).wait_send()
        for block in (OWN, SIDE):
            for copy in mate_copies(block, i):
                copy.wait_send()
                copy.wait_recv()
        for kind in (Q_SAME, Q_OTHER):
            own_message(kind, i).wait_recv()
        for kind in (K, V, Q_SAME, Q_OTHER):
            own_message(kind, i).wait_send()
        for j in range(2):
            relay(j, i).wait_send()
            relay(j, i).wait_recv()

    loop(0, chunks, drain)
    loop(0, at.first_other, lambda i: side_message(Q_OTHER, i).wait_recv())

    def drain_side(i):
        side_message(Q_OTHER, i).wait_send()
        for kind in (K, V, Q_SAME):
            side_message(kind, i).wait_send()
            side_message(kind, i).wait_recv()

    loop(0, at.first, drain_side)


def late_message(at, rows, chunks, stage, targets, f_send, f_recv, kind, i):
    there = chunk_rows(i, (LATE_FAR_MATE if kind == Q_OTHER else LATE_FAR) * rows)
    n = chunks + i
    return send(stage.at[kind, chunk_rows(i), :], targets[kind].at[there, :], f_send.at[kind, n], f_recv.at[kind, n],
                at.far_mate if kind == Q_OTHER else at.far)


def finish(k_held, v_held, far_late, token, q_late, k_late, v_late, answer, f_send, f_recv, r_send, r_recv):
    rows = far_late.shape[1]
    chunks = rows // CHUNK
    at = Place()
    barrier = pltpu.get_barrier_semaphore()
    signal(barrier, at.far)

    @pl.when(at.core == 0)
    def _():
        signal(barrier, at.mate)
        signal(barrier, at.far_mate)

    pl.semaphore_wait(barrier, 1 + 2 * at.core)

    @pl.when(at.core == 1)
    def _():
        signal(answer, at.mate)
        signal(answer, at.far_mate)

    message = functools.partial(late_message, at, rows, 0, far_late, (k_late, v_late, q_late, q_late), f_send, f_recv)

    def relay(j, i, sources=(k_late, v_late)):
        return send(sources[j].at[chunk_rows(i, LATE_FAR * rows), :], (k_late, v_late)[j].at[chunk_rows(i, LATE_FAR_MATE * rows), :],
                    r_send.at[j, i], r_recv.at[j, i], at.mate)

    def start_same(i):
        for kind in (K, V, Q_SAME):
            message(kind, i).start()

    loop(at.first, chunks, start_same)

    @pl.when(at.core == 0)
    def _():
        pl.semaphore_wait(answer, 2)

    loop(at.first, chunks, lambda i: message(Q_OTHER, i).start())

    def relay_held(i):
        for j in range(2):
            relay(j, i, (k_held, v_held)).start()

    loop(0, at.first, relay_held)

    def relay_step(i):
        for j, kind in enumerate((K, V)):
            message(kind, i).wait_recv()
            relay(j, i).start()

    loop(at.first, chunks, relay_step)

    def drain(i):
        message(Q_SAME, i).wait_recv()
        for kind in (K, V, Q_SAME, Q_OTHER):
            message(kind, i).wait_send()

    def drain_relay(i):
        for j in range(2):
            relay(j, i).wait_send()
            relay(j, i).wait_recv()

    loop(0, chunks, drain_relay)
    loop(at.first_other, chunks, lambda i: message(Q_OTHER, i).wait_recv())
    loop(at.first, chunks, drain)


def store_early(q_early, k_early, v_early, q_out, k_out, v_out, token, sems):
    at = Place()
    owners = (at.me, at.side, at.mate, at.across(at.mate), at.far, at.far_mate)
    rows = q_early.shape[0] // len(owners)
    copies = [
        pltpu.make_async_copy(source.at[pl.ds(block * rows, rows), :], target.at[pl.ds(pl.multiple_of(owner * rows, rows), rows), :], sems.at[o, block])
        for o, (source, target) in enumerate(((q_early, q_out), (k_early, k_out), (v_early, v_out)))
        for block, owner in enumerate(owners)
    ]
    for copy in copies:
        copy.start()
    for copy in copies:
        copy.wait()


def store_late(q_held, k_held, v_held, q_late, k_late, v_late, q_in, k_in, v_in, q_out, k_out, v_out, sems):
    at = Place()
    rows = q_late.shape[0] // 2
    held, late, outs = (q_held, k_held, v_held), (q_late, k_late, v_late), (q_out, k_out, v_out)

    def copy(o, block, part, sources):
        first, count = ((0, CHUNK), (CHUNK, rows - 2 * CHUNK), (rows - CHUNK, CHUNK))[part]
        owner = at.across((at.far, at.far_mate)[block])
        return pltpu.make_async_copy(
            sources[o].at[pl.ds(block * rows + first, count), :],
            outs[o].at[pl.ds(pl.multiple_of(owner * rows + first, CHUNK), count), :],
            sems.at[o, block, part],
        )

    for o in range(3):
        for block in range(2):
            relayed = block == LATE_FAR_MATE and o > 0
            copy(o, block, 0, late if relayed else held).start()
            copy(o, block, 2, late).start()
            if relayed:
                copy(o, block, 1, late).start()

    for core in range(2):
        @pl.when(at.core == core)
        def _():
            for o in range(3):
                copy(o, LATE_FAR, 1, held if core else late).start()
            copy(0, LATE_FAR_MATE, 1, late if core else held).start()

    for o in range(3):
        for block in range(2):
            for part in range(3):
                copy(o, block, part, late).wait()


def in_vmem(*arrays):
    return tuple(pltpu.with_memory_space_constraint(array, pltpu.VMEM) for array in arrays)


def solution(mesh):
    group_size = mesh.shape["tp"]

    def local_step(x_rows, norm_gain, w_q, w_k, w_v):
        rows, width = x_rows.shape
        head = w_q.shape[2]
        chunks = rows // CHUNK
        dma = pltpu.SemaphoreType.DMA
        any_space = pl.BlockSpec(memory_space=pl.ANY)
        vmem = pl.BlockSpec(memory_space=pltpu.VMEM)
        hbm = pl.BlockSpec(memory_space=pltpu.HBM)

        def small(**settings):
            return pltpu.CompilerParams(vmem_limit_bytes=1024 * 1024, **settings)

        early = [pltpu.VMEM((6 * rows, head), jnp.bfloat16)] * 3
        late = [pltpu.VMEM((2 * rows, head), jnp.bfloat16)] * 3
        final = [pltpu.HBM((group_size * rows, head), jnp.bfloat16)] * 3

        *gathered, far_late = pl.pallas_call(
            gather,
            out_shape=early + late + [pltpu.VMEM((4, rows, head), jnp.bfloat16)],
            in_specs=[any_space] * 5,
            out_specs=[vmem] * 7,
            scratch_shapes=[
                pltpu.VMEM((rows, width), jnp.bfloat16),
                pltpu.VMEM((rows, width), jnp.bfloat16),
                pltpu.VMEM((width, 4 * head), jnp.bfloat16),
                pltpu.VMEM((width, 4 * head), jnp.bfloat16),
                pltpu.VMEM((4, rows, head), jnp.bfloat16),
                pltpu.VMEM((2 * rows, head), jnp.bfloat16),
                pltpu.VMEM((width,), jnp.float32),
                pltpu.SemaphoreType.REGULAR, dma(()), dma((chunks,)),
                dma((3,)), dma((3,)), dma((3,)), dma((3,)), dma((3,)), dma((3,)), dma((3,)),
                dma((chunks,)), dma((chunks,)), dma((3, 2 * chunks)), dma((3, 2 * chunks)),
                dma((4, 2 * chunks)), dma((4, 2 * chunks)), dma((2, chunks)), dma((2, chunks)),
            ],
            compiler_params=pltpu.CompilerParams(collective_id=0, has_side_effects=True, vmem_limit_bytes=40 * 1024 * 1024),
            name="gather",
        )(x_rows, norm_gain, w_q.reshape(width, head), w_k, w_v)
        *stored, token = pl.pallas_call(
            store_early,
            out_shape=final + [pltpu.HBM((8, 128), jnp.float32)],
            in_specs=[vmem] * 3,
            out_specs=[hbm] * 4,
            scratch_shapes=[dma((3, 6))],
            compiler_params=small(),
            name="store_early",
        )(*in_vmem(*gathered[:3]))
        held = in_vmem(*gathered[3:])
        finished = pl.pallas_call(
            finish,
            out_shape=late,
            in_specs=[vmem] * 3 + [hbm],
            out_specs=[vmem] * 3,
            scratch_shapes=[
                pltpu.SemaphoreType.REGULAR, dma((4, chunks)), dma((4, chunks)), dma((2, chunks)), dma((2, chunks)),
            ],
            compiler_params=small(collective_id=1, has_side_effects=True),
            name="finish",
        )(*held[1:], *in_vmem(far_late), pltpu.with_memory_space_constraint(token, pltpu.HBM))
        outs = pl.pallas_call(
            store_late,
            out_shape=final,
            in_specs=[vmem] * 6 + [hbm] * 3,
            out_specs=[hbm] * 3,
            input_output_aliases={6: 0, 7: 1, 8: 2},
            scratch_shapes=[dma((3, 2, 3))],
            compiler_params=small(),
            name="store_late",
        )(*held, *in_vmem(*finished), *stored)
        return tuple(out[:, None, :] for out in outs)

    return jax.shard_map(local_step, mesh=mesh, in_specs=(P(("dp", "tp"), None), P(None), P(None, "tp", None), P(None, "tp"), P(None, "tp")), out_specs=(P("dp", "tp", None), P("dp", "tp", None), P("dp", "tp", None)), check_vma=False)
```

time: 285 us -> 149 us (0.52)
  waiting for transfers between devices: 176 us -> 0 us
  Pallas kernels: 0 us -> 148 us
  matrix products: 55.8 us -> 0 us
  other arithmetic: 24.9 us -> 0 us
  between operations: 14.1 us -> 0.66 us
  local copies, waits for them, and re-layouts: 12.7 us -> 0 us
    all_gather x1 -> x0, waiting for transfers between devices: 176 us -> none  [local_step(): gathered = lax.all_gather(normed, 'tp', axis=0, tiled=True)]
    pallas_call x0 -> x4, Pallas kernels: none -> 148 us  [the longest x1 124 us: local_step(): pl.pallas_call(gather, out_shape=early + late + [pltpu.VMEM((4, rows, hea...]
    dot_general x3 -> x0, matrix products: 55.8 us -> none  [the longest x1 19.2 us: local_step(): jnp.dot(gathered, w_k, preferred_element_type=jnp.float32)]
    concatenate x2 -> x0, other arithmetic: 15.8 us -> none  [head_pieces(): return jnp.roll(joined, member * piece.shape[1], axis=1)]
    dynamic_slice x2 -> x0, local copies, waits for them, and re-layouts: 12.7 us -> none  [head_pieces(): return jnp.roll(joined, member * piece.shape[1], axis=1)]
    convert_element_type x1 -> x0, other arithmetic: 5.63 us -> none  [local_step(): (x_wide * lax.rsqrt(mean_sq + EPSILON) * norm_gain).astype(jnp.bfloat16)]
    reduce_sum x1 -> x0, other arithmetic: 3.46 us -> none  [local_step(): mean_sq = jnp.mean(x_wide * x_wide, axis=-1, keepdims=True)]
  transfers between devices with their start and end apart: 3 -> 0, of which waited for: 1 -> 0; matrix products, arithmetic and copies ran while one was open for 18% -> 0% of each run, Pallas kernels for 0% -> 0%
where the time goes in v4:
time: 149 us
  Pallas kernels  148 us (99%)
    pallas_call x1, Pallas kernels, local_step(): pl.pallas_call(gather, out_shape=early + late + [pltpu.VMEM((4, rows, hea...  124 us
    pallas_call x1, Pallas kernels, local_step(): pl.pallas_call(finish, out_shape=late, in_specs=[vmem] * 3 + [hbm], out_s...  18.5 us
    pallas_call x1, Pallas kernels, local_step(): pl.pallas_call(store_early, out_shape=final + [pltpu.HBM((8, 128), jnp.fl...  3.76 us

profile of v4, /device:TPU:1, one launch (start us, length us, event | category | flops | bytes accessed | tf_op | source)
XLA Modules:
  0.0 148.7 jit_solution(8644207595204271438)
XLA Ops:
  0.6 123.9 %gather.1 = (bf16[6144,256]{1,0:T(8,128)(2,1)S(1)}, bf16[6144,256]{1,0:T(8,128)(2,1)S(1)}, bf16[6144,256]{1,0:T(8,128)(2,1)S(1)}, bf16[2048,256]{1,0:T(8,128)(2,...) custom-call(bf16[1024,2304]{1,0:T(8,128)(2,1)} %x_hbm.1, ...), custom_call_target="tpu_custom_call" | custom-call | tf_op jit(solution)/shard_map/gather/pallas_call | solution.py:392
  124.5 3.8 %store_early.1 = (bf16[8192,256]{1,0:T(8,128)(2,1)}, bf16[8192,256]{1,0:T(8,128)(2,1)}, bf16[8192,256]{1,0:T(8,128)(2,1)}, f32[8,128]{1,0:T(8,128)}) custom-call(bf16[6144,256]{1,0:T(8,128)(2,1)S(1)} %get-tuple-element.24.q_early, bf16[6144,256]{1,0:T(8,128)(2,1)S(1)} %get-tuple-element.25.k_early, bf16[6144,256]{1,0:T(8,128)(2,1)S(1)} %get-tuple-element.26.v_early), custom_call_target="tpu_custom_call" | custom-call | tf_op jit(solution)/shard_map/store_early/pallas_call | solution.py:413
  128.3 18.5 %finish.1 = (bf16[2048,256]{1,0:T(8,128)(2,1)S(1)}, bf16[2048,256]{1,0:T(8,128)(2,1)S(1)}, bf16[2048,256]{1,0:T(8,128)(2,1)S(1)}) custom-call(bf16[2048,256]{1,0:T(8,128)(2,1)S(1)} %get-tuple-element.21.k_held, bf16[2048,256]{1,0:T(8,128)(2,1)S(1)} %get-tuple-element.22.v_held, bf16[4,1024,256]{2,1,0:T(8,128)(2,1)S(1)} %get-tuple-element.23.far_late, ...), custom_call_target="tpu_custom_call" | custom-call | tf_op jit(solution)/shard_map/finish/pallas_call | solution.py:423
  146.8 1.9 %store_late.1 = (bf16[8192,256]{1,0:T(8,128)(2,1)}, bf16[8192,256]{1,0:T(8,128)(2,1)}, bf16[8192,256]{1,0:T(8,128)(2,1)}) custom-call(bf16[2048,256]{1,0:T(8,128)(2,1)S(1)} %get-tuple-element.20.q_held, bf16[2048,256]{1,0:T(8,128)(2,1)S(1)} %get-tuple-element.21.k_held, ...), custom_call_target="tpu_custom_call", output_to_operand_aliasing={{0}: (6, {}), {1}: (7, {}), {2}: (8, {})} | custom-call | tf_op jit(solution)/shard_map/store_late/pallas_call | solution.py:434

commit v5 on v4

v5 whole, which is shorter than its diff:
```python
import functools

import jax
import jax.numpy as jnp
from jax import lax
from jax.experimental import pallas as pl
from jax.experimental.pallas import tpu as pltpu
from jax.sharding import PartitionSpec as P

EPSILON = 1e-6
CHUNK = 256
SIDE_CHUNK = 128
PIECE = 16

K, V, Q = range(3)
KV, KVQ = pl.ds(0, 2), pl.ds(0, 3)
Q_SAME, Q_OTHER = 2, 3
OWN, SIDE, MATE, MATE_SIDE, FAR, FAR_MATE = range(6)
LATE_FAR, LATE_FAR_MATE = range(2)


class Place:
    def __init__(self):
        self.me = lax.axis_index("tp")
        self.core = lax.rem(self.me, 2)
        self.row = self.me // 4
        self.mate = self.me + 1 - 2 * self.core
        self.side = self.across(self.me)
        self.far = self.me + 2 - 4 * lax.rem(self.me // 2, 2)
        self.far_mate = self.far + 1 - 2 * self.core
        self.first = 1 + 2 * self.core
        self.first_other = 3 - 2 * self.core

    def across(self, device):
        return device + 4 - 8 * (device // 4)


def send(src, dst, send_sem, recv_sem, to):
    return pltpu.make_async_remote_copy(src_ref=src, dst_ref=dst, send_sem=send_sem, recv_sem=recv_sem, device_id={"tp": to})


def signal(sem, to):
    pl.semaphore_signal(sem, inc=1, device_id={"tp": to})


def loop(start, stop, body):
    def step(i, carry):
        body(i)
        return carry

    lax.fori_loop(start, stop, step, 0)


def span(i, size, base=0):
    return pl.ds(pl.multiple_of(base + i * size, size), size)


def side_messages(at, rows, stage, target, send_sems, recv_sems, i):
    return (
        send(stage.at[KVQ, span(i, CHUNK), :], target.at[KVQ, span(i, CHUNK, LATE_FAR * rows), :],
             send_sems.at[0, i], recv_sems.at[0, i], at.far),
        send(stage.at[Q_OTHER, span(i, CHUNK), :], target.at[Q, span(i, CHUNK, LATE_FAR_MATE * rows), :],
             send_sems.at[1, i], recv_sems.at[1, i], at.far_mate),
    )


def gather(x_hbm, gain_hbm, wq_hbm, wk_hbm, wv_hbm, early, late, far_late,
           x_own, x_side, w_own, w_far, far_own, mate_q, gain,
           answer, load_gain, load_x, load_w, mw_send, mw_recv, fw_send, fw_recv, rw_send, rw_recv,
           x_send, x_recv, mo_send, mo_recv, ms_send, ms_recv, fo_send, fo_recv, fs_send, fs_recv, r_send, r_recv):
    rows, width = x_hbm.shape
    head = wq_hbm.shape[1]
    part = wk_hbm.shape[1]
    chunks = rows // CHUNK
    side_chunks = rows // SIDE_CHUNK
    at = Place()
    core = at.core

    barrier = pltpu.get_barrier_semaphore()
    for peer in (at.mate, at.far, at.far_mate):
        signal(barrier, peer)

    @pl.when(at.row == 0)
    def _():
        signal(barrier, at.side)

    q_cols = pl.ds(pl.multiple_of(core * head, head), head)
    k_cols = pl.ds(pl.multiple_of(2 * head + core * part, part), part)
    v_cols = pl.ds(pl.multiple_of(3 * head + core * part, part), part)
    mine = ((wk_hbm, k_cols), (wv_hbm, v_cols), (wq_hbm, q_cols))
    local_w = [pltpu.make_async_copy(src, w_own.at[:, cols], load_w.at[i]) for i, (src, cols) in enumerate(mine)]
    mate_w = [send(w_own.at[:, cols], w_own.at[:, cols], mw_send.at[i], mw_recv.at[i], at.mate) for i, (src, cols) in enumerate(mine)]
    far_w = [send(w_own.at[:, cols], w_far.at[:, cols], fw_send.at[i], fw_recv.at[i], at.far) for i, (src, cols) in enumerate(mine)]
    relay_w = [send(w_far.at[:, cols], w_far.at[:, cols], rw_send.at[i], rw_recv.at[i], at.mate) for i, (src, cols) in enumerate(mine)]

    def load_chunk(i):
        return pltpu.make_async_copy(x_hbm.at[span(i, CHUNK), :], x_own.at[span(i, CHUNK), :], load_x.at[i])

    def side_chunk(i):
        return send(x_hbm.at[span(i, SIDE_CHUNK), :], x_side.at[span(i, SIDE_CHUNK), :], x_send.at[i], x_recv.at[i], at.side)

    for copy in local_w:
        copy.start()
    gain_copy = pltpu.make_async_copy(gain_hbm, gain, load_gain)
    gain_copy.start()
    for i in range(chunks):
        load_chunk(i).start()

    pl.semaphore_wait(barrier, 3 + at.row)
    for i in range(3):
        local_w[i].wait()
        far_w[i].start()

    @pl.when(at.row == 1)
    def _():
        signal(answer, at.side)

    for copy in mate_w:
        copy.start()

    @pl.when(at.row == 0)
    def _():
        pl.semaphore_wait(answer, 1)

    loop(0, side_chunks, lambda i: side_chunk(i).start())

    def normalise(ref, i, size):
        def piece(p, carry):
            here = pl.ds(pl.multiple_of(i * size + p * PIECE, PIECE), PIECE)
            x_wide = ref[here, :].astype(jnp.float32)
            mean_sq = jnp.mean(x_wide * x_wide, axis=-1, keepdims=True)
            ref[here, :] = (x_wide * lax.rsqrt(mean_sq + EPSILON) * gain[...].reshape(1, width)).astype(jnp.bfloat16)
            return carry

        lax.fori_loop(0, size // PIECE, piece, 0, unroll=4)

    def product(ref, here, w, block):
        cols = slice(block * head, (block + 1) * head) if isinstance(block, int) else pl.ds(pl.multiple_of(block * head, head), head)
        return jnp.dot(ref[here, :], w[:, cols], preferred_element_type=jnp.float32).astype(jnp.bfloat16)

    def mate_copies(block, i):
        size, sends, recvs = (SIDE_CHUNK, ms_send, ms_recv) if block == SIDE else (CHUNK, mo_send, mo_recv)
        here, there = span(i, size, block * rows), span(i, size, (MATE + block) * rows)
        return (
            send(early.at[KV, here, :], early.at[KV, there, :], sends.at[0, i], recvs.at[0, i], at.mate),
            send(mate_q.at[here, :], early.at[Q, there, :], sends.at[1, i], recvs.at[1, i], at.mate),
        )

    def near_products(ref, block, i):
        size = SIDE_CHUNK if block == SIDE else CHUNK
        here, source = span(i, size, block * rows), span(i, size)
        early[K, here, :] = product(ref, source, w_own, 2)
        early[V, here, :] = product(ref, source, w_own, 3)
        early[Q, here, :] = product(ref, source, w_own, core)
        mate_q[here, :] = product(ref, source, w_own, 1 - core)
        for copy in mate_copies(block, i):
            copy.start()

    far_columns = {K: 2, V: 3, Q_SAME: core, Q_OTHER: 1 - core}

    def far_products(ref, here, stage, kinds):
        for kind in kinds:
            stage[kind, here, :] = product(ref, here, w_far, far_columns[kind])

    def own_messages(i):
        there = span(i, CHUNK, FAR * rows)
        sources = ((KV, KV, there, at.far), (Q_SAME, Q, there, at.far), (Q_OTHER, Q, span(i, CHUNK, FAR_MATE * rows), at.far_mate))
        return [send(far_own.at[src, span(i, CHUNK), :], early.at[dst, to, :], fo_send.at[j, i], fo_recv.at[j, i], peer)
                for j, (src, dst, to, peer) in enumerate(sources)]

    messages = functools.partial(side_messages, at, rows, far_late, late, fs_send, fs_recv)

    def relay(i):
        return send(early.at[KV, span(i, CHUNK, FAR * rows), :], early.at[KV, span(i, CHUNK, FAR_MATE * rows), :], r_send.at[i], r_recv.at[i], at.mate)

    def own_norm(i):
        load_chunk(i).wait()
        normalise(x_own, i, CHUNK)

    gain_copy.wait()
    loop(0, chunks, own_norm)
    for copy in mate_w:
        copy.wait_recv()
    loop(0, chunks, lambda i: near_products(x_own, OWN, i))

    for i in (0, 1):
        far_w[i].wait_recv()
        relay_w[i].start()
    for i in (0, 1):
        relay_w[i].wait_recv()

    def far_kv_step(i):
        far_products(x_own, span(i, CHUNK), far_own, (K, V))
        own_messages(i)[0].start()

    loop(0, chunks, far_kv_step)
    far_w[2].wait_recv()
    relay_w[2].start()
    relay_w[2].wait_recv()

    def far_q_step(i):
        far_products(x_own, span(i, CHUNK), far_own, (Q_SAME, Q_OTHER))
        for message in own_messages(i)[1:]:
            message.start()

    loop(0, chunks, far_q_step)

    def side_step(i):
        side_chunk(i).wait_recv()
        normalise(x_side, i, SIDE_CHUNK)
        near_products(x_side, SIDE, i)
        far_products(x_side, span(i, SIDE_CHUNK), far_late, (Q_OTHER, K, V, Q_SAME))
        done = lax.rem(i + 1, CHUNK // SIDE_CHUNK) == 0
        n = i // (CHUNK // SIDE_CHUNK)

        @pl.when(done & (n < at.first))
        def _():
            messages(n)[1].start()

        @pl.when(done & (n == at.first - 1))
        def _():
            loop(0, at.first, lambda j: messages(j)[0].start())

    loop(0, side_chunks - 1, side_step)

    def relay_step(i):
        own_messages(i)[0].wait_recv()
        relay(i).start()

    loop(0, chunks, relay_step)

    def drain_own(i):
        for copy in mate_copies(OWN, i):
            copy.wait_send()
            copy.wait_recv()
        for j, message in enumerate(own_messages(i)):
            message.wait_send()
            if j:
                message.wait_recv()
        relay(i).wait_send()
        relay(i).wait_recv()

    loop(0, chunks, drain_own)
    for copies in (mate_w, far_w, relay_w):
        for copy in copies:
            copy.wait_send()

    side_step(side_chunks - 1)

    def drain_side(i):
        side_chunk(i).wait_send()
        for copy in mate_copies(SIDE, i):
            copy.wait_send()
            copy.wait_recv()

    def drain_same(i):
        same, other = messages(i)
        same.wait_send()
        same.wait_recv()
        other.wait_send()

    loop(0, side_chunks, drain_side)
    loop(0, at.first_other, lambda i: messages(i)[1].wait_recv())
    loop(0, at.first, drain_same)


def finish(held, far_late, token, late, answer, fs_send, fs_recv, r_send, r_recv):
    rows = far_late.shape[1]
    chunks = rows // CHUNK
    at = Place()
    barrier = pltpu.get_barrier_semaphore()
    signal(barrier, at.far)

    @pl.when(at.core == 0)
    def _():
        signal(barrier, at.mate)
        signal(barrier, at.far_mate)

    pl.semaphore_wait(barrier, 1 + 2 * at.core)
    messages = functools.partial(side_messages, at, rows, far_late, late, fs_send, fs_recv)
    loop(at.first, chunks, lambda i: messages(i)[0].start())

    @pl.when(at.core == 1)
    def _():
        signal(answer, at.mate)
        signal(answer, at.far_mate)

    @pl.when(at.core == 0)
    def _():
        pl.semaphore_wait(answer, 2)

    loop(at.first, chunks, lambda i: messages(i)[1].start())

    def relay(i, source):
        return send(source.at[KV, span(i, CHUNK, LATE_FAR * rows), :], late.at[KV, span(i, CHUNK, LATE_FAR_MATE * rows), :],
                    r_send.at[i], r_recv.at[i], at.mate)

    loop(0, at.first, lambda i: relay(i, held).start())

    def relay_step(i):
        messages(i)[0].wait_recv()
        relay(i, late).start()

    loop(at.first, chunks, relay_step)

    def drain_relay(i):
        relay(i, late).wait_send()
        relay(i, late).wait_recv()

    def drain(i):
        for message in messages(i):
            message.wait_send()

    loop(0, chunks, drain_relay)
    loop(at.first_other, chunks, lambda i: messages(i)[1].wait_recv())
    loop(at.first, chunks, drain)


def store_early(early, q_out, k_out, v_out, token, sems):
    at = Place()
    owners = (at.me, at.side, at.mate, at.across(at.mate), at.far, at.far_mate)
    rows = early.shape[1] // len(owners)
    copies = [
        pltpu.make_async_copy(early.at[o, pl.ds(block * rows, rows), :], out.at[span(owner, rows), :], sems.at[o, block])
        for o, out in enumerate((k_out, v_out, q_out))
        for block, owner in enumerate(owners)
    ]
    for copy in copies:
        copy.start()
    for copy in copies:
        copy.wait()


def store_late(held, late, q_in, k_in, v_in, q_out, k_out, v_out, sems):
    at = Place()
    rows = late.shape[1] // 2
    outs = (k_out, v_out, q_out)

    def copy(o, block, part, source):
        first, count = ((0, CHUNK), (CHUNK, rows - 2 * CHUNK), (rows - CHUNK, CHUNK))[part]
        owner = at.across((at.far, at.far_mate)[block])
        return pltpu.make_async_copy(
            source.at[o, pl.ds(block * rows + first, count), :],
            outs[o].at[pl.ds(pl.multiple_of(owner * rows + first, CHUNK), count), :],
            sems.at[o, block, part],
        )

    for o in range(3):
        for block in range(2):
            relayed = block == LATE_FAR_MATE and o != Q
            copy(o, block, 0, late if relayed else held).start()
            copy(o, block, 2, late).start()
            if relayed:
                copy(o, block, 1, late).start()

    for core in range(2):
        @pl.when(at.core == core)
        def _():
            for o in range(3):
                copy(o, LATE_FAR, 1, held if core else late).start()
            copy(Q, LATE_FAR_MATE, 1, late if core else held).start()

    for o in range(3):
        for block in range(2):
            for part in range(3):
                copy(o, block, part, late).wait()


def in_vmem(*arrays):
    return tuple(pltpu.with_memory_space_constraint(array, pltpu.VMEM) for array in arrays)


def solution(mesh):
    group_size = mesh.shape["tp"]

    def local_step(x_rows, norm_gain, w_q, w_k, w_v):
        rows, width = x_rows.shape
        head = w_q.shape[2]
        chunks = rows // CHUNK
        dma = pltpu.SemaphoreType.DMA
        any_space = pl.BlockSpec(memory_space=pl.ANY)
        vmem = pl.BlockSpec(memory_space=pltpu.VMEM)
        hbm = pl.BlockSpec(memory_space=pltpu.HBM)

        def small(**settings):
            return pltpu.CompilerParams(vmem_limit_bytes=1024 * 1024, **settings)

        early = pltpu.VMEM((3, 6 * rows, head), jnp.bfloat16)
        late = pltpu.VMEM((3, 2 * rows, head), jnp.bfloat16)
        final = [pltpu.HBM((group_size * rows, head), jnp.bfloat16)] * 3
        side_chunks = rows // SIDE_CHUNK

        gathered, held, far_late = in_vmem(*pl.pallas_call(
            gather,
            out_shape=[early, late, pltpu.VMEM((4, rows, head), jnp.bfloat16)],
            in_specs=[any_space] * 5,
            out_specs=[vmem] * 3,
            scratch_shapes=[
                pltpu.VMEM((rows, width), jnp.bfloat16),
                pltpu.VMEM((rows, width), jnp.bfloat16),
                pltpu.VMEM((width, 4 * head), jnp.bfloat16),
                pltpu.VMEM((width, 4 * head), jnp.bfloat16),
                pltpu.VMEM((4, rows, head), jnp.bfloat16),
                pltpu.VMEM((2 * rows, head), jnp.bfloat16),
                pltpu.VMEM((width,), jnp.float32),
                pltpu.SemaphoreType.REGULAR, dma(()), dma((chunks,)),
                dma((3,)), dma((3,)), dma((3,)), dma((3,)), dma((3,)), dma((3,)), dma((3,)),
                dma((side_chunks,)), dma((side_chunks,)), dma((2, chunks)), dma((2, chunks)), dma((2, side_chunks)), dma((2, side_chunks)),
                dma((3, chunks)), dma((3, chunks)), dma((2, chunks)), dma((2, chunks)), dma((chunks,)), dma((chunks,)),
            ],
            compiler_params=pltpu.CompilerParams(collective_id=0, has_side_effects=True, vmem_limit_bytes=40 * 1024 * 1024),
            name="gather",
        )(x_rows, norm_gain, w_q.reshape(width, head), w_k, w_v))
        *stored, token = pl.pallas_call(
            store_early,
            out_shape=final + [pltpu.HBM((8, 128), jnp.float32)],
            in_specs=[vmem],
            out_specs=[hbm] * 4,
            scratch_shapes=[dma((3, 6))],
            compiler_params=small(),
            name="store_early",
        )(gathered)
        finished = pl.pallas_call(
            finish,
            out_shape=late,
            in_specs=[vmem] * 2 + [hbm],
            out_specs=vmem,
            scratch_shapes=[pltpu.SemaphoreType.REGULAR, dma((2, chunks)), dma((2, chunks)), dma((chunks,)), dma((chunks,))],
            compiler_params=small(collective_id=1, has_side_effects=True),
            name="finish",
        )(held, far_late, pltpu.with_memory_space_constraint(token, pltpu.HBM))
        outs = pl.pallas_call(
            store_late,
            out_shape=final,
            in_specs=[vmem] * 2 + [hbm] * 3,
            out_specs=[hbm] * 3,
            input_output_aliases={2: 0, 3: 1, 4: 2},
            scratch_shapes=[dma((3, 2, 3))],
            compiler_params=small(),
            name="store_late",
        )(held, *in_vmem(finished), *stored)
        return tuple(out[:, None, :] for out in outs)

    return jax.shard_map(local_step, mesh=mesh, in_specs=(P(("dp", "tp"), None), P(None), P(None, "tp", None), P(None, "tp"), P(None, "tp")), out_specs=(P("dp", "tp", None), P("dp", "tp", None), P("dp", "tp", None)), check_vma=False)
```

time: 149 us -> 148 us (level)
  no operation moved by 1% of the time
where the time goes in v5:
time: 148 us
  Pallas kernels  147 us (99%)
    pallas_call x1, Pallas kernels, local_step(): pl.pallas_call(gather, out_shape=[early, late, pltpu.VMEM((4, rows, head)...  126 us
    pallas_call x1, Pallas kernels, local_step(): pl.pallas_call(finish, out_shape=late, in_specs=[vmem] * 2 + [hbm], out_s...  15.6 us
    pallas_call x1, Pallas kernels, local_step(): pl.pallas_call(store_early, out_shape=final + [pltpu.HBM((8, 128), jnp.fl...  3.76 us

profile of v5, /device:TPU:1, one launch (start us, length us, event | category | flops | bytes accessed | tf_op | source)
XLA Modules:
  0.0 147.6 jit_solution(6677754806362339244)
XLA Ops:
  0.6 125.7 %gather.1 = (bf16[3,6144,256]{2,1,0:T(8,128)(2,1)S(1)}, bf16[3,2048,256]{2,1,0:T(8,128)(2,1)S(1)}, bf16[4,1024,256]{2,1,0:T(8,128)(2,1)S(1)}) custom-call(bf16[1024,2304]{1,0:T(8,128)(2,1)} %x_hbm.1, f32[2304]{0:T(1024)} %gain_hbm.1, bf16[2304,256]{1,0:T(8,128)(2,1)} %bitcast.7, bf16[2304,128]{1,0:T(8,128)(2,1)} %wk_hbm.1, bf16[2304,128]{1,0:T(8,128)(2,1)} %wv_hbm.1), custom_call_target="tpu_custom_call" | custom-call | tf_op jit(solution)/shard_map/gather/pallas_call | solution.py:393
  126.4 3.8 %store_early.1 = (bf16[8192,256]{1,0:T(8,128)(2,1)}, bf16[8192,256]{1,0:T(8,128)(2,1)}, bf16[8192,256]{1,0:T(8,128)(2,1)}, f32[8,128]{1,0:T(8,128)}) custom-call(bf16[3,6144,256]{2,1,0:T(8,128)(2,1)S(1)} %get-tuple-element.15.early), custom_call_target="tpu_custom_call" | custom-call | tf_op jit(solution)/shard_map/store_early/pallas_call | solution.py:414
  130.1 15.6 %finish.1.late = bf16[3,2048,256]{2,1,0:T(8,128)(2,1)S(1)} custom-call(bf16[3,2048,256]{2,1,0:T(8,128)(2,1)S(1)} %get-tuple-element.13.held, bf16[4,1024,256]{2,1,0:T(8,128)(2,1)S(1)} %get-tuple-element.14.far_late, f32[8,128]{1,0:T(8,128)} %get-tuple-element.16.token), custom_call_target="tpu_custom_call" | custom-call | tf_op jit(solution)/shard_map/finish/pallas_call | solution.py:423
  145.8 1.8 %store_late.1 = (bf16[8192,256]{1,0:T(8,128)(2,1)}, bf16[8192,256]{1,0:T(8,128)(2,1)}, bf16[8192,256]{1,0:T(8,128)(2,1)}) custom-call(bf16[3,2048,256]{2,1,0:T(8,128)(2,1)S(1)} %get-tuple-element.13.held, bf16[3,2048,256]{2,1,0:T(8,128)(2,1)S(1)} %finish.1.late, ...), custom_call_target="tpu_custom_call", output_to_operand_aliasing={{0}: (2, {}), {1}: (3, {}), {2}: (4, {})} | custom-call | tf_op jit(solution)/shard_map/store_late/pallas_call | solution.py:432

commit v6 on v5

--- a/solution.py
+++ b/solution.py
@@ -55,19 +55,23 @@
     return pl.ds(pl.multiple_of(base + i * size, size), size)
 
 
-def side_messages(at, rows, stage, target, send_sems, recv_sems, i):
-    return (
-        send(stage.at[KVQ, span(i, CHUNK), :], target.at[KVQ, span(i, CHUNK, LATE_FAR * rows), :],
-             send_sems.at[0, i], recv_sems.at[0, i], at.far),
-        send(stage.at[Q_OTHER, span(i, CHUNK), :], target.at[Q, span(i, CHUNK, LATE_FAR_MATE * rows), :],
-             send_sems.at[1, i], recv_sems.at[1, i], at.far_mate),
-    )
+SAME, OTHER = range(2)
+
+
+def side_message(at, rows, stage, target, send_sems, recv_sems, kind, i):
+    src, dst, block, peer = ((KVQ, KVQ, LATE_FAR, at.far), (Q_OTHER, Q, LATE_FAR_MATE, at.far_mate))[kind]
+    return send(stage.at[src, span(i, CHUNK), :], target.at[dst, span(i, CHUNK, block * rows), :], send_sems.at[kind, i], recv_sems.at[kind, i], peer)
+
+
+def late_relay(at, rows, source, target, send_sems, recv_sems, i):
+    return send(source.at[KV, span(i, CHUNK, LATE_FAR * rows), :], target.at[KV, span(i, CHUNK, LATE_FAR_MATE * rows), :],
+                send_sems.at[i], recv_sems.at[i], at.mate)
 
 
 def gather(x_hbm, gain_hbm, wq_hbm, wk_hbm, wv_hbm, early, late, far_late,
            x_own, x_side, w_own, w_far, far_own, mate_q, gain,
-           answer, load_gain, load_x, load_w, mw_send, mw_recv, fw_send, fw_recv, rw_send, rw_recv,
-           x_send, x_recv, mo_send, mo_recv, ms_send, ms_recv, fo_send, fo_recv, fs_send, fs_recv, r_send, r_recv):
+           mate_answer, side_answer, far_answer, load_gain, load_x, load_w, mw_send, mw_recv, fw_send, fw_recv, rw_send, rw_recv,
+           x_send, x_recv, mo_send, mo_recv, ms_send, ms_recv, fo_send, fo_recv, fs_send, fs_recv, r_send, r_recv, lr_send, lr_recv):
     rows, width = x_hbm.shape
     head = wq_hbm.shape[1]
     part = wk_hbm.shape[1]
@@ -77,8 +81,11 @@
     core = at.core
 
     barrier = pltpu.get_barrier_semaphore()
-    for peer in (at.mate, at.far, at.far_mate):
-        signal(barrier, peer)
+    signal(barrier, at.far)
+
+    @pl.when(core == 1)
+    def _():
+        signal(barrier, at.mate)
 
     @pl.when(at.row == 0)
     def _():
@@ -106,21 +113,30 @@
     for i in range(chunks):
         load_chunk(i).start()
 
-    pl.semaphore_wait(barrier, 3 + at.row)
+    pl.semaphore_wait(barrier, 2 - core + at.row)
     for i in range(3):
         local_w[i].wait()
         far_w[i].start()
 
+    @pl.when(core == 0)
+    def _():
+        signal(mate_answer, at.mate)
+
     @pl.when(at.row == 1)
     def _():
-        signal(answer, at.side)
-
+        signal(side_answer, at.side)
+
+    @pl.when(core == 1)
+    def _():
+        pl.semaphore_wait(mate_answer, 1)
+
+    signal(far_answer, at.far)
     for copy in mate_w:
         copy.start()
 
     @pl.when(at.row == 0)
     def _():
-        pl.semaphore_wait(answer, 1)
+        pl.semaphore_wait(side_answer, 1)
 
     loop(0, side_chunks, lambda i: side_chunk(i).start())
 
@@ -162,13 +178,11 @@
         for kind in kinds:
             stage[kind, here, :] = product(ref, here, w_far, far_columns[kind])
 
-    def own_messages(i):
-        there = span(i, CHUNK, FAR * rows)
-        sources = ((KV, KV, there, at.far), (Q_SAME, Q, there, at.far), (Q_OTHER, Q, span(i, CHUNK, FAR_MATE * rows), at.far_mate))
-        return [send(far_own.at[src, span(i, CHUNK), :], early.at[dst, to, :], fo_send.at[j, i], fo_recv.at[j, i], peer)
-                for j, (src, dst, to, peer) in enumerate(sources)]
-
-    messages = functools.partial(side_messages, at, rows, far_late, late, fs_send, fs_recv)
+    def own_message(j, i):
+        src, dst, block, peer = ((KV, KV, FAR, at.far), (Q_SAME, Q, FAR, at.far), (Q_OTHER, Q, FAR_MATE, at.far_mate))[j]
+        return send(far_own.at[src, span(i, CHUNK), :], early.at[dst, span(i, CHUNK, block * rows), :], fo_send.at[j, i], fo_recv.at[j, i], peer)
+
+    message = functools.partial(side_message, at, rows, far_late, late, fs_send, fs_recv)
 
     def relay(i):
         return send(early.at[KV, span(i, CHUNK, FAR * rows), :], early.at[KV, span(i, CHUNK, FAR_MATE * rows), :], r_send.at[i], r_recv.at[i], at.mate)
@@ -191,17 +205,18 @@
 
     def far_kv_step(i):
         far_products(x_own, span(i, CHUNK), far_own, (K, V))
-        own_messages(i)[0].start()
+        own_message(0, i).start()
 
     loop(0, chunks, far_kv_step)
     far_w[2].wait_recv()
     relay_w[2].start()
     relay_w[2].wait_recv()
+    pl.semaphore_wait(far_answer, 1)
 
     def far_q_step(i):
         far_products(x_own, span(i, CHUNK), far_own, (Q_SAME, Q_OTHER))
-        for message in own_messages(i)[1:]:
-            message.start()
+        own_message(1, i).start()
+        own_message(2, i).start()
 
     loop(0, chunks, far_q_step)
 
@@ -215,16 +230,16 @@
 
         @pl.when(done & (n < at.first))
         def _():
-            messages(n)[1].start()
+            message(OTHER, n).start()
 
         @pl.when(done & (n == at.first - 1))
         def _():
-            loop(0, at.first, lambda j: messages(j)[0].start())
+            loop(0, at.first, lambda j: message(SAME, j).start())
 
     loop(0, side_chunks - 1, side_step)
 
     def relay_step(i):
-        own_messages(i)[0].wait_recv()
+        own_message(0, i).wait_recv()
         relay(i).start()
 
     loop(0, chunks, relay_step)
@@ -233,10 +248,10 @@
         for copy in mate_copies(OWN, i):
             copy.wait_send()
             copy.wait_recv()
-        for j, message in enumerate(own_messages(i)):
-            message.wait_send()
-            if j:
-                message.wait_recv()
+        for j in range(3):
+            own_message(j, i).wait_send()
+        for j in (1, 2):
+            own_message(j, i).wait_recv()
         relay(i).wait_send()
         relay(i).wait_recv()
 
@@ -254,14 +269,24 @@
             copy.wait_recv()
 
     def drain_same(i):
-        same, other = messages(i)
-        same.wait_send()
-        same.wait_recv()
-        other.wait_send()
+        message(SAME, i).wait_send()
+        message(SAME, i).wait_recv()
+        message(OTHER, i).wait_send()
 
     loop(0, side_chunks, drain_side)
-    loop(0, at.first_other, lambda i: messages(i)[1].wait_recv())
+    loop(0, at.first_other, lambda i: message(OTHER, i).wait_recv())
     loop(0, at.first, drain_same)
+
+    first_relay = late_relay(at, rows, late, late, lr_send, lr_recv, 0)
+
+    @pl.when(core == 0)
+    def _():
+        first_relay.start()
+        first_relay.wait_send()
+
+    @pl.when(core == 1)
+    def _():
+        first_relay.wait_recv()
 
 
 def finish(held, far_late, token, late, answer, fs_send, fs_recv, r_send, r_recv):
@@ -277,8 +302,8 @@
         signal(barrier, at.far_mate)
 
     pl.semaphore_wait(barrier, 1 + 2 * at.core)
-    messages = functools.partial(side_messages, at, rows, far_late, late, fs_send, fs_recv)
-    loop(at.first, chunks, lambda i: messages(i)[0].start())
+    message = functools.partial(side_message, at, rows, far_late, late, fs_send, fs_recv)
+    loop(at.first, chunks, lambda i: message(SAME, i).start())
 
     @pl.when(at.core == 1)
     def _():
@@ -289,81 +314,78 @@
     def _():
         pl.semaphore_wait(answer, 2)
 
-    loop(at.first, chunks, lambda i: messages(i)[1].start())
-
-    def relay(i, source):
-        return send(source.at[KV, span(i, CHUNK, LATE_FAR * rows), :], late.at[KV, span(i, CHUNK, LATE_FAR_MATE * rows), :],
-                    r_send.at[i], r_recv.at[i], at.mate)
-
-    loop(0, at.first, lambda i: relay(i, held).start())
+    loop(at.first, chunks, lambda i: message(OTHER, i).start())
+
+    def relay(i, source=late):
+        return late_relay(at, rows, source, late, r_send, r_recv, i)
+
+    loop(1 - at.core, at.first, lambda i: relay(i, held).start())
 
     def relay_step(i):
-        messages(i)[0].wait_recv()
-        relay(i, late).start()
+        message(SAME, i).wait_recv()
+        relay(i).start()
 
     loop(at.first, chunks, relay_step)
-
-    def drain_relay(i):
-        relay(i, late).wait_send()
-        relay(i, late).wait_recv()
+    loop(at.core, chunks, lambda i: relay(i).wait_recv())
+    loop(1 - at.core, chunks, lambda i: relay(i).wait_send())
+    loop(at.first_other, chunks, lambda i: message(OTHER, i).wait_recv())
 
     def drain(i):
-        for message in messages(i):
-            message.wait_send()
-
-    loop(0, chunks, drain_relay)
-    loop(at.first_other, chunks, lambda i: messages(i)[1].wait_recv())
+        message(SAME, i).wait_send()
+        message(OTHER, i).wait_send()
+
     loop(at.first, chunks, drain)
 
 
-def store_early(early, q_out, k_out, v_out, token, sems):
-    at = Place()
-    owners = (at.me, at.side, at.mate, at.across(at.mate), at.far, at.far_mate)
-    rows = early.shape[1] // len(owners)
-    copies = [
-        pltpu.make_async_copy(early.at[o, pl.ds(block * rows, rows), :], out.at[span(owner, rows), :], sems.at[o, block])
-        for o, out in enumerate((k_out, v_out, q_out))
-        for block, owner in enumerate(owners)
-    ]
+def late_chunks(core, held):
+    first, other, relayed = (1, 3, 0) if core == 0 else (3, 1, 1)
+    spans = [(o, LATE_FAR, first) for o in (K, V, Q)] + [(Q, LATE_FAR_MATE, other)] + [(o, LATE_FAR_MATE, relayed) for o in (K, V)]
+    return [(o, block, 0, n) if held else (o, block, n, None) for o, block, n in spans]
+
+
+def store_chunks(at, source, outs, sems, core, held):
+    rows = source.shape[1] // 2
+    owners = tuple(at.across(device) for device in (at.far, at.far_mate))
+    copies = []
+    for j, (o, block, start, count) in enumerate(late_chunks(core, held)):
+        count = (rows // CHUNK - start if count is None else count) * CHUNK
+        if count:
+            copies.append(pltpu.make_async_copy(
+                source.at[o, pl.ds(block * rows + start * CHUNK, count), :],
+                outs[o].at[pl.ds(pl.multiple_of(owners[block] * rows + start * CHUNK, CHUNK), count), :],
+                sems.at[j],
+            ))
+    return copies
+
+
+def run(copies):
     for copy in copies:
         copy.start()
     for copy in copies:
         copy.wait()
 
 
-def store_late(held, late, q_in, k_in, v_in, q_out, k_out, v_out, sems):
+def store_early(early, held, q_out, k_out, v_out, token, sems, held_sems):
     at = Place()
-    rows = late.shape[1] // 2
+    owners = (at.me, at.side, at.mate, at.across(at.mate), at.far, at.far_mate)
+    rows = early.shape[1] // len(owners)
     outs = (k_out, v_out, q_out)
-
-    def copy(o, block, part, source):
-        first, count = ((0, CHUNK), (CHUNK, rows - 2 * CHUNK), (rows - CHUNK, CHUNK))[part]
-        owner = at.across((at.far, at.far_mate)[block])
-        return pltpu.make_async_copy(
-            source.at[o, pl.ds(block * rows + first, count), :],
-            outs[o].at[pl.ds(pl.multiple_of(owner * rows + first, CHUNK), count), :],
-            sems.at[o, block, part],
-        )
-
-    for o in range(3):
-        for block in range(2):
-            relayed = block == LATE_FAR_MATE and o != Q
-            copy(o, block, 0, late if relayed else held).start()
-            copy(o, block, 2, late).start()
-            if relayed:
-                copy(o, block, 1, late).start()
-
     for core in range(2):
         @pl.when(at.core == core)
         def _():
-            for o in range(3):
-                copy(o, LATE_FAR, 1, held if core else late).start()
-            copy(Q, LATE_FAR_MATE, 1, late if core else held).start()
-
-    for o in range(3):
-        for block in range(2):
-            for part in range(3):
-                copy(o, block, part, late).wait()
+            run([
+                pltpu.make_async_copy(early.at[o, pl.ds(block * rows, rows), :], out.at[span(owner, rows), :], sems.at[o, block])
+                for o, out in enumerate(outs)
+                for block, owner in enumerate(owners)
+            ] + store_chunks(at, held, outs, held_sems, core, True))
+
+
+def store_late(late, q_in, k_in, v_in, q_out, k_out, v_out, sems):
+    at = Place()
+    for core in range(2):
+        @pl.when(at.core == core)
+        def _():
+            run(store_chunks(at, late, (k_out, v_out, q_out), sems, core, False))
 
 
 def in_vmem(*arrays):
@@ -403,10 +425,10 @@
                 pltpu.VMEM((4, rows, head), jnp.bfloat16),
                 pltpu.VMEM((2 * rows, head), jnp.bfloat16),
                 pltpu.VMEM((width,), jnp.float32),
-                pltpu.SemaphoreType.REGULAR, dma(()), dma((chunks,)),
+                *[pltpu.SemaphoreType.REGULAR] * 3, dma(()), dma((chunks,)),
                 dma((3,)), dma((3,)), dma((3,)), dma((3,)), dma((3,)), dma((3,)), dma((3,)),
                 dma((side_chunks,)), dma((side_chunks,)), dma((2, chunks)), dma((2, chunks)), dma((2, side_chunks)), dma((2, side_chunks)),
-                dma((3, chunks)), dma((3, chunks)), dma((2, chunks)), dma((2, chunks)), dma((chunks,)), dma((chunks,)),
+                dma((3, chunks)), dma((3, chunks)), dma((2, chunks)), dma((2, chunks)), dma((chunks,)), dma((chunks,)), dma((1,)), dma((1,)),
             ],
             compiler_params=pltpu.CompilerParams(collective_id=0, has_side_effects=True, vmem_limit_bytes=40 * 1024 * 1024),
             name="gather",
@@ -414,12 +436,12 @@
         *stored, token = pl.pallas_call(
             store_early,
             out_shape=final + [pltpu.HBM((8, 128), jnp.float32)],
-            in_specs=[vmem],
+            in_specs=[vmem] * 2,
             out_specs=[hbm] * 4,
-            scratch_shapes=[dma((3, 6))],
+            scratch_shapes=[dma((3, 6)), dma((6,))],
             compiler_params=small(),
             name="store_early",
-        )(gathered)
+        )(gathered, held)
         finished = pl.pallas_call(
             finish,
             out_shape=late,
@@ -432,13 +454,13 @@
         outs = pl.pallas_call(
             store_late,
             out_shape=final,
-            in_specs=[vmem] * 2 + [hbm] * 3,
+            in_specs=[vmem] + [hbm] * 3,
             out_specs=[hbm] * 3,
-            input_output_aliases={2: 0, 3: 1, 4: 2},
-            scratch_shapes=[dma((3, 2, 3))],
+            input_output_aliases={1: 0, 2: 1, 3: 2},
+            scratch_shapes=[dma((6,))],
             compiler_params=small(),
             name="store_late",
-        )(held, *in_vmem(finished), *stored)
+        )(*in_vmem(finished), *stored)
         return tuple(out[:, None, :] for out in outs)
 
     return jax.shard_map(local_step, mesh=mesh, in_specs=(P(("dp", "tp"), None), P(None), P(None, "tp", None), P(None, "tp"), P(None, "tp")), out_specs=(P("dp", "tp", None), P("dp", "tp", None), P("dp", "tp", None)), check_vma=False)

time: 148 us -> 147 us (level)
  no operation moved by 1% of the time
where the time goes in v6:
time: 147 us
  Pallas kernels  146 us (99%)
    pallas_call x1, Pallas kernels, local_step(): pl.pallas_call(gather, out_shape=[early, late, pltpu.VMEM((4, rows, head)...  124 us
    pallas_call x1, Pallas kernels, local_step(): pl.pallas_call(finish, out_shape=late, in_specs=[vmem] * 2 + [hbm], out_s...  16.5 us
    pallas_call x1, Pallas kernels, local_step(): pl.pallas_call(store_early, out_shape=final + [pltpu.HBM((8, 128), jnp.fl...  4.28 us

profile of v6, /device:TPU:1, one launch (start us, length us, event | category | flops | bytes accessed | tf_op | source)
XLA Modules:
  0.0 147.0 jit_solution(6791144314589054154)
XLA Ops:
  0.6 124.3 %gather.1 = (bf16[3,6144,256]{2,1,0:T(8,128)(2,1)S(1)}, bf16[3,2048,256]{2,1,0:T(8,128)(2,1)S(1)}, bf16[4,1024,256]{2,1,0:T(8,128)(2,1)S(1)}) custom-call(bf16[1024,2304]{1,0:T(8,128)(2,1)} %x_hbm.1, f32[2304]{0:T(1024)} %gain_hbm.1, bf16[2304,256]{1,0:T(8,128)(2,1)} %bitcast.7, bf16[2304,128]{1,0:T(8,128)(2,1)} %wk_hbm.1, bf16[2304,128]{1,0:T(8,128)(2,1)} %wv_hbm.1), custom_call_target="tpu_custom_call" | custom-call | tf_op jit(solution)/shard_map/gather/pallas_call | solution.py:415
  124.9 4.3 %store_early.1 = (bf16[8192,256]{1,0:T(8,128)(2,1)}, bf16[8192,256]{1,0:T(8,128)(2,1)}, bf16[8192,256]{1,0:T(8,128)(2,1)}, f32[8,128]{1,0:T(8,128)}) custom-call(bf16[3,6144,256]{2,1,0:T(8,128)(2,1)S(1)} %get-tuple-element.15.early, bf16[3,2048,256]{2,1,0:T(8,128)(2,1)S(1)} %get-tuple-element.13.held), custom_call_target="tpu_custom_call" | custom-call | tf_op jit(solution)/shard_map/store_early/pallas_call | solution.py:436
  129.2 16.5 %finish.1.late = bf16[3,2048,256]{2,1,0:T(8,128)(2,1)S(1)} custom-call(bf16[3,2048,256]{2,1,0:T(8,128)(2,1)S(1)} %get-tuple-element.13.held, bf16[4,1024,256]{2,1,0:T(8,128)(2,1)S(1)} %get-tuple-element.14.far_late, f32[8,128]{1,0:T(8,128)} %get-tuple-element.16.token), custom_call_target="tpu_custom_call" | custom-call | tf_op jit(solution)/shard_map/finish/pallas_call | solution.py:445
  145.8 1.2 store_late.1

commit v7 on v6

--- a/solution.py
+++ b/solution.py
@@ -70,7 +70,7 @@
 
 def gather(x_hbm, gain_hbm, wq_hbm, wk_hbm, wv_hbm, early, late, far_late,
            x_own, x_side, w_own, w_far, far_own, mate_q, gain,
-           mate_answer, side_answer, far_answer, load_gain, load_x, load_w, mw_send, mw_recv, fw_send, fw_recv, rw_send, rw_recv,
+           mate_answer, side_answer, far_answer, load_gain, load_x, lw_sem, mw_send, mw_recv, fw_send, fw_recv, rw_send, rw_recv,
            x_send, x_recv, mo_send, mo_recv, ms_send, ms_recv, fo_send, fo_recv, fs_send, fs_recv, r_send, r_recv, lr_send, lr_recv):
     rows, width = x_hbm.shape
     head = wq_hbm.shape[1]
@@ -94,11 +94,20 @@
     q_cols = pl.ds(pl.multiple_of(core * head, head), head)
     k_cols = pl.ds(pl.multiple_of(2 * head + core * part, part), part)
     v_cols = pl.ds(pl.multiple_of(3 * head + core * part, part), part)
-    mine = ((wk_hbm, k_cols), (wv_hbm, v_cols), (wq_hbm, q_cols))
-    local_w = [pltpu.make_async_copy(src, w_own.at[:, cols], load_w.at[i]) for i, (src, cols) in enumerate(mine)]
-    mate_w = [send(w_own.at[:, cols], w_own.at[:, cols], mw_send.at[i], mw_recv.at[i], at.mate) for i, (src, cols) in enumerate(mine)]
-    far_w = [send(w_own.at[:, cols], w_far.at[:, cols], fw_send.at[i], fw_recv.at[i], at.far) for i, (src, cols) in enumerate(mine)]
-    relay_w = [send(w_far.at[:, cols], w_far.at[:, cols], rw_send.at[i], rw_recv.at[i], at.mate) for i, (src, cols) in enumerate(mine)]
+    lead = width // 4
+    mine = (
+        (wk_hbm, pl.ds(0, lead), k_cols),
+        (wk_hbm, pl.ds(lead, width - lead), k_cols),
+        (wv_hbm, pl.ds(0, width), v_cols),
+        (wq_hbm, pl.ds(0, width), q_cols),
+    )
+    load_w, mate_w, far_w, relay_w = [], [], [], []
+    for i, (src, depth, cols) in enumerate(mine):
+        near_part, far_part = w_own.at[depth, cols], w_far.at[depth, cols]
+        load_w.append(pltpu.make_async_copy(src.at[depth, :], near_part, lw_sem.at[i]))
+        mate_w.append(send(near_part, near_part, mw_send.at[i], mw_recv.at[i], at.mate))
+        far_w.append(send(near_part, far_part, fw_send.at[i], fw_recv.at[i], at.far))
+        relay_w.append(send(far_part, far_part, rw_send.at[i], rw_recv.at[i], at.mate))
 
     def load_chunk(i):
         return pltpu.make_async_copy(x_hbm.at[span(i, CHUNK), :], x_own.at[span(i, CHUNK), :], load_x.at[i])
@@ -106,17 +115,18 @@
     def side_chunk(i):
         return send(x_hbm.at[span(i, SIDE_CHUNK), :], x_side.at[span(i, SIDE_CHUNK), :], x_send.at[i], x_recv.at[i], at.side)
 
-    for copy in local_w:
+    for copy in load_w:
         copy.start()
+
+    pl.semaphore_wait(barrier, 2 - core + at.row)
+    for load, copy in zip(load_w, far_w):
+        load.wait()
+        copy.start()
+
     gain_copy = pltpu.make_async_copy(gain_hbm, gain, load_gain)
     gain_copy.start()
     for i in range(chunks):
         load_chunk(i).start()
-
-    pl.semaphore_wait(barrier, 2 - core + at.row)
-    for i in range(3):
-        local_w[i].wait()
-        far_w[i].start()
 
     @pl.when(core == 0)
     def _():
@@ -197,20 +207,20 @@
         copy.wait_recv()
     loop(0, chunks, lambda i: near_products(x_own, OWN, i))
 
-    for i in (0, 1):
-        far_w[i].wait_recv()
-        relay_w[i].start()
-    for i in (0, 1):
-        relay_w[i].wait_recv()
+    for arrived, onward in zip(far_w[:3], relay_w[:3]):
+        arrived.wait_recv()
+        onward.start()
+    for copy in relay_w[:3]:
+        copy.wait_recv()
 
     def far_kv_step(i):
         far_products(x_own, span(i, CHUNK), far_own, (K, V))
         own_message(0, i).start()
 
     loop(0, chunks, far_kv_step)
-    far_w[2].wait_recv()
-    relay_w[2].start()
-    relay_w[2].wait_recv()
+    far_w[3].wait_recv()
+    relay_w[3].start()
+    relay_w[3].wait_recv()
     pl.semaphore_wait(far_answer, 1)
 
     def far_q_step(i):
@@ -426,7 +436,7 @@
                 pltpu.VMEM((2 * rows, head), jnp.bfloat16),
                 pltpu.VMEM((width,), jnp.float32),
                 *[pltpu.SemaphoreType.REGULAR] * 3, dma(()), dma((chunks,)),
-                dma((3,)), dma((3,)), dma((3,)), dma((3,)), dma((3,)), dma((3,)), dma((3,)),
+                *[dma((4,))] * 7,
                 dma((side_chunks,)), dma((side_chunks,)), dma((2, chunks)), dma((2, chunks)), dma((2, side_chunks)), dma((2, side_chunks)),
                 dma((3, chunks)), dma((3, chunks)), dma((2, chunks)), dma((2, chunks)), dma((chunks,)), dma((chunks,)), dma((1,)), dma((1,)),
             ],

time: 147 us -> 147 us (level)
  no operation moved by 1% of the time
where the time goes in v7:
time: 147 us; the launch traced here: 146 us
  Pallas kernels  146 us (99%)
    pallas_call x1, Pallas kernels, local_step(): pl.pallas_call(gather, out_shape=[early, late, pltpu.VMEM((4, rows, head)...  124 us
    pallas_call x1, Pallas kernels, local_step(): pl.pallas_call(finish, out_shape=late, in_specs=[vmem] * 2 + [hbm], out_s...  16.5 us
    pallas_call x1, Pallas kernels, local_step(): pl.pallas_call(store_early, out_shape=final + [pltpu.HBM((8, 128), jnp.fl...  4.28 us

profile of v7, /device:TPU:1, one launch (start us, length us, event | category | flops | bytes accessed | tf_op | source)
XLA Modules:
  0.0 146.5 jit_solution(7314654836205133282)
XLA Ops:
  0.6 123.8 %gather.1 = (bf16[3,6144,256]{2,1,0:T(8,128)(2,1)S(1)}, bf16[3,2048,256]{2,1,0:T(8,128)(2,1)S(1)}, bf16[4,1024,256]{2,1,0:T(8,128)(2,1)S(1)}) custom-call(bf16[1024,2304]{1,0:T(8,128)(2,1)} %x_hbm.1, f32[2304]{0:T(1024)} %gain_hbm.1, bf16[2304,256]{1,0:T(8,128)(2,1)} %bitcast.7, bf16[2304,128]{1,0:T(8,128)(2,1)} %wk_hbm.1, bf16[2304,128]{1,0:T(8,128)(2,1)} %wv_hbm.1), custom_call_target="tpu_custom_call" | custom-call | tf_op jit(solution)/shard_map/gather/pallas_call | solution.py:425
  124.4 4.3 %store_early.1 = (bf16[8192,256]{1,0:T(8,128)(2,1)}, bf16[8192,256]{1,0:T(8,128)(2,1)}, bf16[8192,256]{1,0:T(8,128)(2,1)}, f32[8,128]{1,0:T(8,128)}) custom-call(bf16[3,6144,256]{2,1,0:T(8,128)(2,1)S(1)} %get-tuple-element.15.early, bf16[3,2048,256]{2,1,0:T(8,128)(2,1)S(1)} %get-tuple-element.13.held), custom_call_target="tpu_custom_call" | custom-call | tf_op jit(solution)/shard_map/store_early/pallas_call | solution.py:446
  128.7 16.5 %finish.1.late = bf16[3,2048,256]{2,1,0:T(8,128)(2,1)S(1)} custom-call(bf16[3,2048,256]{2,1,0:T(8,128)(2,1)S(1)} %get-tuple-element.13.held, bf16[4,1024,256]{2,1,0:T(8,128)(2,1)S(1)} %get-tuple-element.14.far_late, f32[8,128]{1,0:T(8,128)} %get-tuple-element.16.token), custom_call_target="tpu_custom_call" | custom-call | tf_op jit(solution)/shard_map/finish/pallas_call | solution.py:455
  145.2 1.2 store_late.1

commit v8 on v7

--- a/solution.py
+++ b/solution.py
@@ -28,8 +28,8 @@
         self.side = self.across(self.me)
         self.far = self.me + 2 - 4 * lax.rem(self.me // 2, 2)
         self.far_mate = self.far + 1 - 2 * self.core
-        self.first = 1 + 2 * self.core
-        self.first_other = 3 - 2 * self.core
+        self.first = FIRST[0] + (FIRST[1] - FIRST[0]) * self.core
+        self.first_other = FIRST[0] + FIRST[1] - self.first
 
     def across(self, device):
         return device + 4 - 8 * (device // 4)
@@ -51,20 +51,27 @@
     lax.fori_loop(start, stop, step, 0)
 
 
-def span(i, size, base=0):
-    return pl.ds(pl.multiple_of(base + i * size, size), size)
+def span(i, size, base=0, count=1):
+    return pl.ds(pl.multiple_of(base + i * size, size), count * size)
+
+
+def by_core(at, body):
+    for core in range(2):
+        pl.when(at.core == core)(functools.partial(body, core))
 
 
 SAME, OTHER = range(2)
-
-
-def side_message(at, rows, stage, target, send_sems, recv_sems, kind, i):
+FIRST = (1, 3)
+
+
+def side_message(at, rows, stage, target, send_sems, recv_sems, kind, i, count=1):
     src, dst, block, peer = ((KVQ, KVQ, LATE_FAR, at.far), (Q_OTHER, Q, LATE_FAR_MATE, at.far_mate))[kind]
-    return send(stage.at[src, span(i, CHUNK), :], target.at[dst, span(i, CHUNK, block * rows), :], send_sems.at[kind, i], recv_sems.at[kind, i], peer)
-
-
-def late_relay(at, rows, source, target, send_sems, recv_sems, i):
-    return send(source.at[KV, span(i, CHUNK, LATE_FAR * rows), :], target.at[KV, span(i, CHUNK, LATE_FAR_MATE * rows), :],
+    return send(stage.at[src, span(i, CHUNK, 0, count), :], target.at[dst, span(i, CHUNK, block * rows, count), :],
+                send_sems.at[kind, i], recv_sems.at[kind, i], peer)
+
+
+def late_relay(at, rows, source, target, send_sems, recv_sems, i, count=1):
+    return send(source.at[KV, span(i, CHUNK, LATE_FAR * rows, count), :], target.at[KV, span(i, CHUNK, LATE_FAR_MATE * rows, count), :],
                 send_sems.at[i], recv_sems.at[i], at.mate)
 
 
@@ -244,7 +251,7 @@
 
         @pl.when(done & (n == at.first - 1))
         def _():
-            loop(0, at.first, lambda j: message(SAME, j).start())
+            by_core(at, lambda c: message(SAME, 0, FIRST[c]).start())
 
     loop(0, side_chunks - 1, side_step)
 
@@ -278,25 +285,22 @@
             copy.wait_send()
             copy.wait_recv()
 
-    def drain_same(i):
-        message(SAME, i).wait_send()
-        message(SAME, i).wait_recv()
-        message(OTHER, i).wait_send()
-
     loop(0, side_chunks, drain_side)
     loop(0, at.first_other, lambda i: message(OTHER, i).wait_recv())
-    loop(0, at.first, drain_same)
-
-    first_relay = late_relay(at, rows, late, late, lr_send, lr_recv, 0)
-
-    @pl.when(core == 0)
-    def _():
-        first_relay.start()
-        first_relay.wait_send()
-
-    @pl.when(core == 1)
-    def _():
-        first_relay.wait_recv()
+    loop(0, at.first, lambda i: message(OTHER, i).wait_send())
+
+    def close(c):
+        same = message(SAME, 0, FIRST[c])
+        same.wait_recv()
+        onward = late_relay(at, rows, late, late, lr_send, lr_recv, 0, FIRST[0])
+        if c == 0:
+            onward.start()
+            onward.wait_send()
+        else:
+            onward.wait_recv()
+        same.wait_send()
+
+    by_core(at, close)
 
 
 def finish(held, far_late, token, late, answer, fs_send, fs_recv, r_send, r_recv):
@@ -313,42 +317,38 @@
 
     pl.semaphore_wait(barrier, 1 + 2 * at.core)
     message = functools.partial(side_message, at, rows, far_late, late, fs_send, fs_recv)
-    loop(at.first, chunks, lambda i: message(SAME, i).start())
-
-    @pl.when(at.core == 1)
-    def _():
-        signal(answer, at.mate)
-        signal(answer, at.far_mate)
-
-    @pl.when(at.core == 0)
-    def _():
-        pl.semaphore_wait(answer, 2)
-
-    loop(at.first, chunks, lambda i: message(OTHER, i).start())
-
-    def relay(i, source=late):
-        return late_relay(at, rows, source, late, r_send, r_recv, i)
-
-    loop(1 - at.core, at.first, lambda i: relay(i, held).start())
-
-    def relay_step(i):
-        message(SAME, i).wait_recv()
-        relay(i).start()
-
-    loop(at.first, chunks, relay_step)
-    loop(at.core, chunks, lambda i: relay(i).wait_recv())
-    loop(1 - at.core, chunks, lambda i: relay(i).wait_send())
-    loop(at.first_other, chunks, lambda i: message(OTHER, i).wait_recv())
-
-    def drain(i):
-        message(SAME, i).wait_send()
-        message(OTHER, i).wait_send()
-
-    loop(at.first, chunks, drain)
+    relay = functools.partial(late_relay, at, rows)
+
+    def body(c):
+        first, other_first = FIRST[c], FIRST[1 - c]
+        same, other = (message(kind, first, chunks - first) for kind in (SAME, OTHER))
+        same.start()
+        relays = [relay(held, late, r_send, r_recv, 0, first)] if c else []
+        if c:
+            signal(answer, at.mate)
+            signal(answer, at.far_mate)
+        else:
+            pl.semaphore_wait(answer, 2)
+        other.start()
+        for copy in relays:
+            copy.start()
+        same.wait_recv()
+        relays.append(relay(late, late, r_send, r_recv, first, chunks - first))
+        relays[-1].start()
+        if c == 0:
+            relay(held, late, r_send, r_recv, 0, other_first).wait_recv()
+        relay(late, late, r_send, r_recv, other_first, chunks - other_first).wait_recv()
+        for copy in relays:
+            copy.wait_send()
+        same.wait_send()
+        message(OTHER, other_first, chunks - other_first).wait_recv()
+        other.wait_send()
+
+    by_core(at, body)
 
 
 def late_chunks(core, held):
-    first, other, relayed = (1, 3, 0) if core == 0 else (3, 1, 1)
+    first, other, relayed = FIRST[core], FIRST[1 - core], core * FIRST[0]
     spans = [(o, LATE_FAR, first) for o in (K, V, Q)] + [(Q, LATE_FAR_MATE, other)] + [(o, LATE_FAR_MATE, relayed) for o in (K, V)]
     return [(o, block, 0, n) if held else (o, block, n, None) for o, block, n in spans]
 

time: 147 us -> 147 us (level)
  no operation moved by 1% of the time
where the time goes in v8:
time: 147 us; the launch traced here: 146 us
  Pallas kernels  146 us (99%)
    pallas_call x1, Pallas kernels, local_step(): pl.pallas_call(gather, out_shape=[early, late, pltpu.VMEM((4, rows, head)...  124 us
    pallas_call x1, Pallas kernels, local_step(): pl.pallas_call(finish, out_shape=late, in_specs=[vmem] * 2 + [hbm], out_s...  16.5 us
    pallas_call x1, Pallas kernels, local_step(): pl.pallas_call(store_early, out_shape=final + [pltpu.HBM((8, 128), jnp.fl...  4.28 us

profile of v8, /device:TPU:1, one launch (start us, length us, event | category | flops | bytes accessed | tf_op | source)
XLA Modules:
  0.0 146.5 jit_solution(3624012143678019000)
XLA Ops:
  0.6 123.8 %gather.1 = (bf16[3,6144,256]{2,1,0:T(8,128)(2,1)S(1)}, bf16[3,2048,256]{2,1,0:T(8,128)(2,1)S(1)}, bf16[4,1024,256]{2,1,0:T(8,128)(2,1)S(1)}) custom-call(bf16[1024,2304]{1,0:T(8,128)(2,1)} %x_hbm.1, f32[2304]{0:T(1024)} %gain_hbm.1, bf16[2304,256]{1,0:T(8,128)(2,1)} %bitcast.7, bf16[2304,128]{1,0:T(8,128)(2,1)} %wk_hbm.1, bf16[2304,128]{1,0:T(8,128)(2,1)} %wv_hbm.1), custom_call_target="tpu_custom_call" | custom-call | tf_op jit(solution)/shard_map/gather/pallas_call | solution.py:425
  124.4 4.3 %store_early.1 = (bf16[8192,256]{1,0:T(8,128)(2,1)}, bf16[8192,256]{1,0:T(8,128)(2,1)}, bf16[8192,256]{1,0:T(8,128)(2,1)}, f32[8,128]{1,0:T(8,128)}) custom-call(bf16[3,6144,256]{2,1,0:T(8,128)(2,1)S(1)} %get-tuple-element.15.early, bf16[3,2048,256]{2,1,0:T(8,128)(2,1)S(1)} %get-tuple-element.13.held), custom_call_target="tpu_custom_call" | custom-call | tf_op jit(solution)/shard_map/store_early/pallas_call | solution.py:446
  128.7 16.5 %finish.1.late = bf16[3,2048,256]{2,1,0:T(8,128)(2,1)S(1)} custom-call(bf16[3,2048,256]{2,1,0:T(8,128)(2,1)S(1)} %get-tuple-element.13.held, bf16[4,1024,256]{2,1,0:T(8,128)(2,1)S(1)} %get-tuple-element.14.far_late, f32[8,128]{1,0:T(8,128)} %get-tuple-element.16.token), custom_call_target="tpu_custom_call" | custom-call | tf_op jit(solution)/shard_map/finish/pallas_call | solution.py:455
  145.2 1.2 store_late.1

commit v9 on v8

--- a/solution.py
+++ b/solution.py
@@ -60,12 +60,17 @@
         pl.when(at.core == core)(functools.partial(body, core))
 
 
-SAME, OTHER = range(2)
+SAME, OTHER, SAME_KV, SAME_Q = range(4)
 FIRST = (1, 3)
 
 
 def side_message(at, rows, stage, target, send_sems, recv_sems, kind, i, count=1):
-    src, dst, block, peer = ((KVQ, KVQ, LATE_FAR, at.far), (Q_OTHER, Q, LATE_FAR_MATE, at.far_mate))[kind]
+    src, dst, block, peer = {
+        SAME: (KVQ, KVQ, LATE_FAR, at.far),
+        SAME_KV: (KV, KV, LATE_FAR, at.far),
+        SAME_Q: (Q_SAME, Q, LATE_FAR, at.far),
+        OTHER: (Q_OTHER, Q, LATE_FAR_MATE, at.far_mate),
+    }[kind]
     return send(stage.at[src, span(i, CHUNK, 0, count), :], target.at[dst, span(i, CHUNK, block * rows, count), :],
                 send_sems.at[kind, i], recv_sems.at[kind, i], peer)
 
@@ -321,28 +326,39 @@
 
     def body(c):
         first, other_first = FIRST[c], FIRST[1 - c]
-        same, other = (message(kind, first, chunks - first) for kind in (SAME, OTHER))
-        same.start()
-        relays = [relay(held, late, r_send, r_recv, 0, first)] if c else []
-        if c:
+        here = functools.partial(message, i=first, count=chunks - first)
+        if c == 0:
+            same = [here(SAME)]
+            other = [message(OTHER, first), message(OTHER, first + 1, chunks - first - 1)]
+            other_arrives = [message(OTHER, other_first, chunks - other_first)]
+            relays = []
+            relays_arrive = [relay(held, late, r_send, r_recv, 0, other_first)]
+        else:
+            same = [here(SAME_KV), here(SAME_Q)]
+            other = [here(OTHER)]
+            other_arrives = [message(OTHER, other_first), message(OTHER, other_first + 1, chunks - other_first - 1)]
+            relays = [relay(held, late, r_send, r_recv, 0, first)]
+            relays_arrive = []
+        onward = relay(late, late, r_send, r_recv, first, chunks - first)
+        relays_arrive.append(relay(late, late, r_send, r_recv, other_first, chunks - other_first))
+
+        same[0].start()
+        if c == 0:
+            pl.semaphore_wait(answer, 2)
+        else:
             signal(answer, at.mate)
             signal(answer, at.far_mate)
-        else:
-            pl.semaphore_wait(answer, 2)
-        other.start()
-        for copy in relays:
+        for copy in other + relays:
             copy.start()
-        same.wait_recv()
-        relays.append(relay(late, late, r_send, r_recv, first, chunks - first))
-        relays[-1].start()
-        if c == 0:
-            relay(held, late, r_send, r_recv, 0, other_first).wait_recv()
-        relay(late, late, r_send, r_recv, other_first, chunks - other_first).wait_recv()
-        for copy in relays:
+        same[0].wait_recv()
+        onward.start()
+        if c == 1:
+            other_arrives[0].wait_recv()
+            same[1].start()
+        for copy in relays_arrive + other_arrives[c:] + same[1:]:
+            copy.wait_recv()
+        for copy in relays + [onward] + same + other:
             copy.wait_send()
-        same.wait_send()
-        message(OTHER, other_first, chunks - other_first).wait_recv()
-        other.wait_send()
 
     by_core(at, body)
 
@@ -457,7 +473,7 @@
             out_shape=late,
             in_specs=[vmem] * 2 + [hbm],
             out_specs=vmem,
-            scratch_shapes=[pltpu.SemaphoreType.REGULAR, dma((2, chunks)), dma((2, chunks)), dma((chunks,)), dma((chunks,))],
+            scratch_shapes=[pltpu.SemaphoreType.REGULAR, dma((4, chunks)), dma((4, chunks)), dma((chunks,)), dma((chunks,))],
             compiler_params=small(collective_id=1, has_side_effects=True),
             name="finish",
         )(held, far_late, pltpu.with_memory_space_constraint(token, pltpu.HBM))

time: 147 us -> 147 us (level)
  no operation moved by 1% of the time
where the time goes in v9:
time: 147 us
  Pallas kernels  146 us (99%)
    pallas_call x1, Pallas kernels, local_step(): pl.pallas_call(gather, out_shape=[early, late, pltpu.VMEM((4, rows, head)...  124 us
    pallas_call x1, Pallas kernels, local_step(): pl.pallas_call(finish, out_shape=late, in_specs=[vmem] * 2 + [hbm], out_s...  16.7 us
    pallas_call x1, Pallas kernels, local_step(): pl.pallas_call(store_early, out_shape=final + [pltpu.HBM((8, 128), jnp.fl...  4.28 us

profile of v9, /device:TPU:1, one launch (start us, length us, event | category | flops | bytes accessed | tf_op | source)
XLA Modules:
  0.0 146.6 jit_solution(2267966253068650695)
XLA Ops:
  0.6 123.8 %gather.1 = (bf16[3,6144,256]{2,1,0:T(8,128)(2,1)S(1)}, bf16[3,2048,256]{2,1,0:T(8,128)(2,1)S(1)}, bf16[4,1024,256]{2,1,0:T(8,128)(2,1)S(1)}) custom-call(bf16[1024,2304]{1,0:T(8,128)(2,1)} %x_hbm.1, f32[2304]{0:T(1024)} %gain_hbm.1, bf16[2304,256]{1,0:T(8,128)(2,1)} %bitcast.7, bf16[2304,128]{1,0:T(8,128)(2,1)} %wk_hbm.1, bf16[2304,128]{1,0:T(8,128)(2,1)} %wv_hbm.1), custom_call_target="tpu_custom_call" | custom-call | tf_op jit(solution)/shard_map/gather/pallas_call | solution.py:441
  124.4 4.3 %store_early.1 = (bf16[8192,256]{1,0:T(8,128)(2,1)}, bf16[8192,256]{1,0:T(8,128)(2,1)}, bf16[8192,256]{1,0:T(8,128)(2,1)}, f32[8,128]{1,0:T(8,128)}) custom-call(bf16[3,6144,256]{2,1,0:T(8,128)(2,1)S(1)} %get-tuple-element.15.early, bf16[3,2048,256]{2,1,0:T(8,128)(2,1)S(1)} %get-tuple-element.13.held), custom_call_target="tpu_custom_call" | custom-call | tf_op jit(solution)/shard_map/store_early/pallas_call | solution.py:462
  128.7 16.7 %finish.1.late = bf16[3,2048,256]{2,1,0:T(8,128)(2,1)S(1)} custom-call(bf16[3,2048,256]{2,1,0:T(8,128)(2,1)S(1)} %get-tuple-element.13.held, bf16[4,1024,256]{2,1,0:T(8,128)(2,1)S(1)} %get-tuple-element.14.far_late, f32[8,128]{1,0:T(8,128)} %get-tuple-element.16.token), custom_call_target="tpu_custom_call" | custom-call | tf_op jit(solution)/shard_map/finish/pallas_call | solution.py:471
  145.4 1.2 store_late.1

commit v10 on v9

--- a/solution.py
+++ b/solution.py
@@ -11,6 +11,7 @@
 CHUNK = 256
 SIDE_CHUNK = 128
 PIECE = 16
+LEAD = 128
 
 K, V, Q = range(3)
 KV, KVQ = pl.ds(0, 2), pl.ds(0, 3)
@@ -64,15 +65,16 @@
 FIRST = (1, 3)
 
 
-def side_message(at, rows, stage, target, send_sems, recv_sems, kind, i, count=1):
+def side_message(at, rows, stage, target, send_sems, recv_sems, kind, i, count=1, size=CHUNK, slot=None):
     src, dst, block, peer = {
         SAME: (KVQ, KVQ, LATE_FAR, at.far),
         SAME_KV: (KV, KV, LATE_FAR, at.far),
         SAME_Q: (Q_SAME, Q, LATE_FAR, at.far),
         OTHER: (Q_OTHER, Q, LATE_FAR_MATE, at.far_mate),
     }[kind]
-    return send(stage.at[src, span(i, CHUNK, 0, count), :], target.at[dst, span(i, CHUNK, block * rows, count), :],
-                send_sems.at[kind, i], recv_sems.at[kind, i], peer)
+    slot = i if slot is None else slot
+    return send(stage.at[src, span(i, size, 0, count), :], target.at[dst, span(i, size, block * rows, count), :],
+                send_sems.at[kind, slot], recv_sems.at[kind, slot], peer)
 
 
 def late_relay(at, rows, source, target, send_sems, recv_sems, i, count=1):
@@ -327,16 +329,18 @@
     def body(c):
         first, other_first = FIRST[c], FIRST[1 - c]
         here = functools.partial(message, i=first, count=chunks - first)
+        lead = FIRST[0] * CHUNK // LEAD
+        others_of_core_0 = [message(OTHER, lead, 1, LEAD, 0), message(OTHER, lead + 1, (chunks - FIRST[0]) * CHUNK // LEAD - 1, LEAD, 1)]
         if c == 0:
             same = [here(SAME)]
-            other = [message(OTHER, first), message(OTHER, first + 1, chunks - first - 1)]
+            other = others_of_core_0
             other_arrives = [message(OTHER, other_first, chunks - other_first)]
             relays = []
             relays_arrive = [relay(held, late, r_send, r_recv, 0, other_first)]
         else:
             same = [here(SAME_KV), here(SAME_Q)]
             other = [here(OTHER)]
-            other_arrives = [message(OTHER, other_first), message(OTHER, other_first + 1, chunks - other_first - 1)]
+            other_arrives = others_of_core_0
             relays = [relay(held, late, r_send, r_recv, 0, first)]
             relays_arrive = []
         onward = relay(late, late, r_send, r_recv, first, chunks - first)

time: 147 us -> 147 us (level)
  no operation moved by 1% of the time
where the time goes in v10:
time: 147 us
  Pallas kernels  146 us (99%)
    pallas_call x1, Pallas kernels, local_step(): pl.pallas_call(gather, out_shape=[early, late, pltpu.VMEM((4, rows, head)...  124 us
    pallas_call x1, Pallas kernels, local_step(): pl.pallas_call(finish, out_shape=late, in_specs=[vmem] * 2 + [hbm], out_s...  16.7 us
    pallas_call x1, Pallas kernels, local_step(): pl.pallas_call(store_early, out_shape=final + [pltpu.HBM((8, 128), jnp.fl...  4.28 us

profile of v10, /device:TPU:1, one launch (start us, length us, event | category | flops | bytes accessed | tf_op | source)
XLA Modules:
  0.0 146.6 jit_solution(8163456995906274825)
XLA Ops:
  0.6 123.8 %gather.1 = (bf16[3,6144,256]{2,1,0:T(8,128)(2,1)S(1)}, bf16[3,2048,256]{2,1,0:T(8,128)(2,1)S(1)}, bf16[4,1024,256]{2,1,0:T(8,128)(2,1)S(1)}) custom-call(bf16[1024,2304]{1,0:T(8,128)(2,1)} %x_hbm.1, f32[2304]{0:T(1024)} %gain_hbm.1, bf16[2304,256]{1,0:T(8,128)(2,1)} %bitcast.7, bf16[2304,128]{1,0:T(8,128)(2,1)} %wk_hbm.1, bf16[2304,128]{1,0:T(8,128)(2,1)} %wv_hbm.1), custom_call_target="tpu_custom_call" | custom-call | tf_op jit(solution)/shard_map/gather/pallas_call | solution.py:445
  124.4 4.3 %store_early.1 = (bf16[8192,256]{1,0:T(8,128)(2,1)}, bf16[8192,256]{1,0:T(8,128)(2,1)}, bf16[8192,256]{1,0:T(8,128)(2,1)}, f32[8,128]{1,0:T(8,128)}) custom-call(bf16[3,6144,256]{2,1,0:T(8,128)(2,1)S(1)} %get-tuple-element.15.early, bf16[3,2048,256]{2,1,0:T(8,128)(2,1)S(1)} %get-tuple-element.13.held), custom_call_target="tpu_custom_call" | custom-call | tf_op jit(solution)/shard_map/store_early/pallas_call | solution.py:466
  128.7 16.7 %finish.1.late = bf16[3,2048,256]{2,1,0:T(8,128)(2,1)S(1)} custom-call(bf16[3,2048,256]{2,1,0:T(8,128)(2,1)S(1)} %get-tuple-element.13.held, bf16[4,1024,256]{2,1,0:T(8,128)(2,1)S(1)} %get-tuple-element.14.far_late, f32[8,128]{1,0:T(8,128)} %get-tuple-element.16.token), custom_call_target="tpu_custom_call" | custom-call | tf_op jit(solution)/shard_map/finish/pallas_call | solution.py:475
  145.4 1.2 store_late.1

commit v11 on v8

--- a/solution.py
+++ b/solution.py
@@ -11,6 +11,7 @@
 CHUNK = 256
 SIDE_CHUNK = 128
 PIECE = 16
+DETOUR = 32
 
 K, V, Q = range(3)
 KV, KVQ = pl.ds(0, 2), pl.ds(0, 3)
@@ -76,8 +77,8 @@
 
 
 def gather(x_hbm, gain_hbm, wq_hbm, wk_hbm, wv_hbm, early, late, far_late,
-           x_own, x_side, w_own, w_far, far_own, mate_q, gain,
-           mate_answer, side_answer, far_answer, load_gain, load_x, lw_sem, mw_send, mw_recv, fw_send, fw_recv, rw_send, rw_recv,
+           x_own, x_side, w_own, w_far, far_own, mate_q, gain, detoured,
+           mate_answer, side_answer, far_answer, aside_send, aside_recv, across_send, across_recv, load_gain, load_x, lw_sem, mw_send, mw_recv, fw_send, fw_recv, rw_send, rw_recv,
            x_send, x_recv, mo_send, mo_recv, ms_send, ms_recv, fo_send, fo_recv, fs_send, fs_recv, r_send, r_recv, lr_send, lr_recv):
     rows, width = x_hbm.shape
     head = wq_hbm.shape[1]
@@ -106,7 +107,8 @@
         (wk_hbm, pl.ds(0, lead), k_cols),
         (wk_hbm, pl.ds(lead, width - lead), k_cols),
         (wv_hbm, pl.ds(0, width), v_cols),
-        (wq_hbm, pl.ds(0, width), q_cols),
+        (wq_hbm, pl.ds(0, width - DETOUR), q_cols),
+        (wq_hbm, pl.ds(width - DETOUR, DETOUR), q_cols),
     )
     load_w, mate_w, far_w, relay_w = [], [], [], []
     for i, (src, depth, cols) in enumerate(mine):
@@ -125,24 +127,34 @@
     for copy in load_w:
         copy.start()
 
+    last = w_own.at[mine[4][1], q_cols]
+    aside = send(last, detoured, aside_send, aside_recv, at.side)
+    across = send(detoured, w_far.at[mine[4][1], q_cols], across_send, across_recv, at.across(at.far))
+
     pl.semaphore_wait(barrier, 2 - core + at.row)
-    for load, copy in zip(load_w, far_w):
+    for load, copy in zip(load_w[:3], far_w[:3]):
         load.wait()
         copy.start()
+    for load in load_w[3:]:
+        load.wait()
+
+    @pl.when(at.row == 0)
+    def _():
+        far_w[3].start()
+
+    @pl.when(core == 0)
+    def _():
+        signal(mate_answer, at.mate)
+
+    @pl.when(at.row == 1)
+    def _():
+        signal(side_answer, at.side)
 
     gain_copy = pltpu.make_async_copy(gain_hbm, gain, load_gain)
     gain_copy.start()
     for i in range(chunks):
         load_chunk(i).start()
 
-    @pl.when(core == 0)
-    def _():
-        signal(mate_answer, at.mate)
-
-    @pl.when(at.row == 1)
-    def _():
-        signal(side_answer, at.side)
-
     @pl.when(core == 1)
     def _():
         pl.semaphore_wait(mate_answer, 1)
@@ -154,8 +166,16 @@
     @pl.when(at.row == 0)
     def _():
         pl.semaphore_wait(side_answer, 1)
+        aside.start()
 
     loop(0, side_chunks, lambda i: side_chunk(i).start())
+
+    @pl.when(at.row == 1)
+    def _():
+        aside.wait_recv()
+        across.start()
+        for copy in far_w[3:]:
+            copy.start()
 
     def normalise(ref, i, size):
         def piece(p, carry):
@@ -227,7 +247,18 @@
     loop(0, chunks, far_kv_step)
     far_w[3].wait_recv()
     relay_w[3].start()
-    relay_w[3].wait_recv()
+
+    @pl.when(at.row == 0)
+    def _():
+        across.wait_recv()
+
+    @pl.when(at.row == 1)
+    def _():
+        far_w[4].wait_recv()
+
+    relay_w[4].start()
+    for copy in relay_w[3:]:
+        copy.wait_recv()
     pl.semaphore_wait(far_answer, 1)
 
     def far_q_step(i):
@@ -273,9 +304,18 @@
         relay(i).wait_recv()
 
     loop(0, chunks, drain_own)
-    for copies in (mate_w, far_w, relay_w):
+    for copies in (mate_w, far_w[:4], relay_w):
         for copy in copies:
             copy.wait_send()
+
+    @pl.when(at.row == 0)
+    def _():
+        aside.wait_send()
+
+    @pl.when(at.row == 1)
+    def _():
+        across.wait_send()
+        far_w[4].wait_send()
 
     side_step(side_chunks - 1)
 
@@ -435,8 +475,9 @@
                 pltpu.VMEM((4, rows, head), jnp.bfloat16),
                 pltpu.VMEM((2 * rows, head), jnp.bfloat16),
                 pltpu.VMEM((width,), jnp.float32),
-                *[pltpu.SemaphoreType.REGULAR] * 3, dma(()), dma((chunks,)),
-                *[dma((4,))] * 7,
+                pltpu.VMEM((DETOUR, head), jnp.bfloat16),
+                *[pltpu.SemaphoreType.REGULAR] * 3, *[dma(())] * 5, dma((chunks,)),
+                *[dma((5,))] * 7,
                 dma((side_chunks,)), dma((side_chunks,)), dma((2, chunks)), dma((2, chunks)), dma((2, side_chunks)), dma((2, side_chunks)),
                 dma((3, chunks)), dma((3, chunks)), dma((2, chunks)), dma((2, chunks)), dma((chunks,)), dma((chunks,)), dma((1,)), dma((1,)),
             ],

time: 147 us -> 146 us (level)
  no operation moved by 1% of the time
where the time goes in v11:
time: 146 us
  Pallas kernels  145 us (99%)
    pallas_call x1, Pallas kernels, local_step(): pl.pallas_call(gather, out_shape=[early, late, pltpu.VMEM((4, rows, head)...  123 us
    pallas_call x1, Pallas kernels, local_step(): pl.pallas_call(finish, out_shape=late, in_specs=[vmem] * 2 + [hbm], out_s...  16.5 us
    pallas_call x1, Pallas kernels, local_step(): pl.pallas_call(store_early, out_shape=final + [pltpu.HBM((8, 128), jnp.fl...  4.28 us

profile of v11, /device:TPU:1, one launch (start us, length us, event | category | flops | bytes accessed | tf_op | source)
XLA Modules:
  0.0 146.1 jit_solution(12063961335220033511)
XLA Ops:
  0.6 123.4 %gather.1 = (bf16[3,6144,256]{2,1,0:T(8,128)(2,1)S(1)}, bf16[3,2048,256]{2,1,0:T(8,128)(2,1)S(1)}, bf16[4,1024,256]{2,1,0:T(8,128)(2,1)S(1)}) custom-call(bf16[1024,2304]{1,0:T(8,128)(2,1)} %x_hbm.1, f32[2304]{0:T(1024)} %gain_hbm.1, bf16[2304,256]{1,0:T(8,128)(2,1)} %bitcast.7, bf16[2304,128]{1,0:T(8,128)(2,1)} %wk_hbm.1, bf16[2304,128]{1,0:T(8,128)(2,1)} %wv_hbm.1), custom_call_target="tpu_custom_call" | custom-call | tf_op jit(solution)/shard_map/gather/pallas_call | solution.py:465
  124.1 4.3 %store_early.1 = (bf16[8192,256]{1,0:T(8,128)(2,1)}, bf16[8192,256]{1,0:T(8,128)(2,1)}, bf16[8192,256]{1,0:T(8,128)(2,1)}, f32[8,128]{1,0:T(8,128)}) custom-call(bf16[3,6144,256]{2,1,0:T(8,128)(2,1)S(1)} %get-tuple-element.15.early, bf16[3,2048,256]{2,1,0:T(8,128)(2,1)S(1)} %get-tuple-element.13.held), custom_call_target="tpu_custom_call" | custom-call | tf_op jit(solution)/shard_map/store_early/pallas_call | solution.py:487
  128.3 16.5 %finish.1.late = bf16[3,2048,256]{2,1,0:T(8,128)(2,1)S(1)} custom-call(bf16[3,2048,256]{2,1,0:T(8,128)(2,1)S(1)} %get-tuple-element.13.held, bf16[4,1024,256]{2,1,0:T(8,128)(2,1)S(1)} %get-tuple-element.14.far_late, f32[8,128]{1,0:T(8,128)} %get-tuple-element.16.token), custom_call_target="tpu_custom_call" | custom-call | tf_op jit(solution)/shard_map/finish/pallas_call | solution.py:496
  144.9 1.2 store_late.1

commit v12 on v11

--- a/solution.py
+++ b/solution.py
@@ -65,15 +65,14 @@
 FIRST = (1, 3)
 
 
-def side_message(at, rows, stage, target, send_sems, recv_sems, kind, i, count=1):
+def side_message(at, rows, stage, target, send_sem, recv_sem, kind, i, count=1):
     src, dst, block, peer = ((KVQ, KVQ, LATE_FAR, at.far), (Q_OTHER, Q, LATE_FAR_MATE, at.far_mate))[kind]
-    return send(stage.at[src, span(i, CHUNK, 0, count), :], target.at[dst, span(i, CHUNK, block * rows, count), :],
-                send_sems.at[kind, i], recv_sems.at[kind, i], peer)
-
-
-def late_relay(at, rows, source, target, send_sems, recv_sems, i, count=1):
+    return send(stage.at[src, span(i, CHUNK, 0, count), :], target.at[dst, span(i, CHUNK, block * rows, count), :], send_sem, recv_sem, peer)
+
+
+def late_relay(at, rows, source, target, send_sem, recv_sem, i, count=1):
     return send(source.at[KV, span(i, CHUNK, LATE_FAR * rows, count), :], target.at[KV, span(i, CHUNK, LATE_FAR_MATE * rows, count), :],
-                send_sems.at[i], recv_sems.at[i], at.mate)
+                send_sem, recv_sem, at.mate)
 
 
 def gather(x_hbm, gain_hbm, wq_hbm, wk_hbm, wv_hbm, early, late, far_late,
@@ -102,7 +101,7 @@
     q_cols = pl.ds(pl.multiple_of(core * head, head), head)
     k_cols = pl.ds(pl.multiple_of(2 * head + core * part, part), part)
     v_cols = pl.ds(pl.multiple_of(3 * head + core * part, part), part)
-    lead = width // 4
+    lead = 6 * PIECE
     mine = (
         (wk_hbm, pl.ds(0, lead), k_cols),
         (wk_hbm, pl.ds(lead, width - lead), k_cols),
@@ -219,7 +218,8 @@
         src, dst, block, peer = ((KV, KV, FAR, at.far), (Q_SAME, Q, FAR, at.far), (Q_OTHER, Q, FAR_MATE, at.far_mate))[j]
         return send(far_own.at[src, span(i, CHUNK), :], early.at[dst, span(i, CHUNK, block * rows), :], fo_send.at[j, i], fo_recv.at[j, i], peer)
 
-    message = functools.partial(side_message, at, rows, far_late, late, fs_send, fs_recv)
+    def message(kind, i, count=1):
+        return side_message(at, rows, far_late, late, fs_send.at[kind, i], fs_recv.at[kind, i], kind, i, count)
 
     def relay(i):
         return send(early.at[KV, span(i, CHUNK, FAR * rows), :], early.at[KV, span(i, CHUNK, FAR_MATE * rows), :], r_send.at[i], r_recv.at[i], at.mate)
@@ -228,10 +228,10 @@
         load_chunk(i).wait()
         normalise(x_own, i, CHUNK)
 
+    for copy in mate_w:
+        copy.wait_recv()
     gain_copy.wait()
     loop(0, chunks, own_norm)
-    for copy in mate_w:
-        copy.wait_recv()
     loop(0, chunks, lambda i: near_products(x_own, OWN, i))
 
     for arrived, onward in zip(far_w[:3], relay_w[:3]):
@@ -343,7 +343,7 @@
     by_core(at, close)
 
 
-def finish(held, far_late, token, late, answer, fs_send, fs_recv, r_send, r_recv):
+def finish(held, far_late, token, late, answer, send_sem, same_recv, other_recv, relay_recv):
     rows = far_late.shape[1]
     chunks = rows // CHUNK
     at = Place()
@@ -356,33 +356,32 @@
         signal(barrier, at.far_mate)
 
     pl.semaphore_wait(barrier, 1 + 2 * at.core)
-    message = functools.partial(side_message, at, rows, far_late, late, fs_send, fs_recv)
-    relay = functools.partial(late_relay, at, rows)
+    def message(kind, i, count):
+        return side_message(at, rows, far_late, late, send_sem, (same_recv, other_recv)[kind], kind, i, count)
+
+    def relay(source, i, count):
+        return late_relay(at, rows, source, late, send_sem, relay_recv, i, count)
 
     def body(c):
         first, other_first = FIRST[c], FIRST[1 - c]
         same, other = (message(kind, first, chunks - first) for kind in (SAME, OTHER))
         same.start()
-        relays = [relay(held, late, r_send, r_recv, 0, first)] if c else []
         if c:
             signal(answer, at.mate)
             signal(answer, at.far_mate)
         else:
             pl.semaphore_wait(answer, 2)
         other.start()
-        for copy in relays:
-            copy.start()
+        if c:
+            relay(held, 0, first).start()
         same.wait_recv()
-        relays.append(relay(late, late, r_send, r_recv, first, chunks - first))
-        relays[-1].start()
-        if c == 0:
-            relay(held, late, r_send, r_recv, 0, other_first).wait_recv()
-        relay(late, late, r_send, r_recv, other_first, chunks - other_first).wait_recv()
-        for copy in relays:
-            copy.wait_send()
-        same.wait_send()
+        relay(late, first, chunks - first).start()
+        arrived = chunks if c == 0 else chunks - other_first
+        relay(late, 0, arrived).wait_recv()
         message(OTHER, other_first, chunks - other_first).wait_recv()
-        other.wait_send()
+        sent = 4 * (chunks - first) + 2 * (chunks if c else chunks - first)
+        everything = late.at[KVQ, span(0, CHUNK, 0, sent // 3), :]
+        pltpu.make_async_copy(everything, everything, send_sem).wait()
 
     by_core(at, body)
 
@@ -393,17 +392,17 @@
     return [(o, block, 0, n) if held else (o, block, n, None) for o, block, n in spans]
 
 
-def store_chunks(at, source, outs, sems, core, held):
+def store_chunks(at, source, outs, sem, core, held):
     rows = source.shape[1] // 2
     owners = tuple(at.across(device) for device in (at.far, at.far_mate))
     copies = []
-    for j, (o, block, start, count) in enumerate(late_chunks(core, held)):
+    for o, block, start, count in late_chunks(core, held):
         count = (rows // CHUNK - start if count is None else count) * CHUNK
         if count:
             copies.append(pltpu.make_async_copy(
                 source.at[o, pl.ds(block * rows + start * CHUNK, count), :],
                 outs[o].at[pl.ds(pl.multiple_of(owners[block] * rows + start * CHUNK, CHUNK), count), :],
-                sems.at[j],
+                sem,
             ))
     return copies
 
@@ -415,7 +414,7 @@
         copy.wait()
 
 
-def store_early(early, held, q_out, k_out, v_out, token, sems, held_sems):
+def store_early(early, held, q_out, k_out, v_out, token, sem):
     at = Place()
     owners = (at.me, at.side, at.mate, at.across(at.mate), at.far, at.far_mate)
     rows = early.shape[1] // len(owners)
@@ -424,18 +423,18 @@
         @pl.when(at.core == core)
         def _():
             run([
-                pltpu.make_async_copy(early.at[o, pl.ds(block * rows, rows), :], out.at[span(owner, rows), :], sems.at[o, block])
+                pltpu.make_async_copy(early.at[o, pl.ds(block * rows, rows), :], out.at[span(owner, rows), :], sem)
                 for o, out in enumerate(outs)
                 for block, owner in enumerate(owners)
-            ] + store_chunks(at, held, outs, held_sems, core, True))
-
-
-def store_late(late, q_in, k_in, v_in, q_out, k_out, v_out, sems):
+            ] + store_chunks(at, held, outs, sem, core, True))
+
+
+def store_late(late, q_in, k_in, v_in, q_out, k_out, v_out, sem):
     at = Place()
     for core in range(2):
         @pl.when(at.core == core)
         def _():
-            run(store_chunks(at, late, (k_out, v_out, q_out), sems, core, False))
+            run(store_chunks(at, late, (k_out, v_out, q_out), sem, core, False))
 
 
 def in_vmem(*arrays):
@@ -479,7 +478,7 @@
                 *[pltpu.SemaphoreType.REGULAR] * 3, *[dma(())] * 5, dma((chunks,)),
                 *[dma((5,))] * 7,
                 dma((side_chunks,)), dma((side_chunks,)), dma((2, chunks)), dma((2, chunks)), dma((2, side_chunks)), dma((2, side_chunks)),
-                dma((3, chunks)), dma((3, chunks)), dma((2, chunks)), dma((2, chunks)), dma((chunks,)), dma((chunks,)), dma((1,)), dma((1,)),
+                dma((3, chunks)), dma((3, chunks)), dma((2, chunks)), dma((2, chunks)), dma((chunks,)), dma((chunks,)), dma(()), dma(()),
             ],
             compiler_params=pltpu.CompilerParams(collective_id=0, has_side_effects=True, vmem_limit_bytes=40 * 1024 * 1024),
             name="gather",
@@ -489,7 +488,7 @@
             out_shape=final + [pltpu.HBM((8, 128), jnp.float32)],
             in_specs=[vmem] * 2,
             out_specs=[hbm] * 4,
-            scratch_shapes=[dma((3, 6)), dma((6,))],
+            scratch_shapes=[dma(())],
             compiler_params=small(),
             name="store_early",
         )(gathered, held)
@@ -498,7 +497,7 @@
             out_shape=late,
             in_specs=[vmem] * 2 + [hbm],
             out_specs=vmem,
-            scratch_shapes=[pltpu.SemaphoreType.REGULAR, dma((2, chunks)), dma((2, chunks)), dma((chunks,)), dma((chunks,))],
+            scratch_shapes=[pltpu.SemaphoreType.REGULAR] + [dma(())] * 4,
             compiler_params=small(collective_id=1, has_side_effects=True),
             name="finish",
         )(held, far_late, pltpu.with_memory_space_constraint(token, pltpu.HBM))
@@ -508,7 +507,7 @@
             in_specs=[vmem] + [hbm] * 3,
             out_specs=[hbm] * 3,
             input_output_aliases={1: 0, 2: 1, 3: 2},
-            scratch_shapes=[dma((6,))],
+            scratch_shapes=[dma(())],
             compiler_params=small(),
             name="store_late",
         )(*in_vmem(finished), *stored)

time: 146 us -> 146 us (level)
  no operation moved by 1% of the time
where the time goes in v12:
time: 146 us
  Pallas kernels  145 us (99%)
    pallas_call x1, Pallas kernels, local_step(): pl.pallas_call(gather, out_shape=[early, late, pltpu.VMEM((4, rows, head)...  124 us
    pallas_call x1, Pallas kernels, local_step(): pl.pallas_call(finish, out_shape=late, in_specs=[vmem] * 2 + [hbm], out_s...  16.3 us
    pallas_call x1, Pallas kernels, local_step(): pl.pallas_call(store_early, out_shape=final + [pltpu.HBM((8, 128), jnp.fl...  4.08 us

profile of v12, /device:TPU:1, one launch (start us, length us, event | category | flops | bytes accessed | tf_op | source)
XLA Modules:
  0.0 145.8 jit_solution(12426820121645223822)
XLA Ops:
  0.6 123.6 %gather.1 = (bf16[3,6144,256]{2,1,0:T(8,128)(2,1)S(1)}, bf16[3,2048,256]{2,1,0:T(8,128)(2,1)S(1)}, bf16[4,1024,256]{2,1,0:T(8,128)(2,1)S(1)}) custom-call(bf16[1024,2304]{1,0:T(8,128)(2,1)} %x_hbm.1, f32[2304]{0:T(1024)} %gain_hbm.1, bf16[2304,256]{1,0:T(8,128)(2,1)} %bitcast.7, bf16[2304,128]{1,0:T(8,128)(2,1)} %wk_hbm.1, bf16[2304,128]{1,0:T(8,128)(2,1)} %wv_hbm.1), custom_call_target="tpu_custom_call" | custom-call | tf_op jit(solution)/shard_map/gather/pallas_call | solution.py:464
  124.2 4.1 %store_early.1 = (bf16[8192,256]{1,0:T(8,128)(2,1)}, bf16[8192,256]{1,0:T(8,128)(2,1)}, bf16[8192,256]{1,0:T(8,128)(2,1)}, f32[8,128]{1,0:T(8,128)}) custom-call(bf16[3,6144,256]{2,1,0:T(8,128)(2,1)S(1)} %get-tuple-element.15.early, bf16[3,2048,256]{2,1,0:T(8,128)(2,1)S(1)} %get-tuple-element.13.held), custom_call_target="tpu_custom_call" | custom-call | tf_op jit(solution)/shard_map/store_early/pallas_call | solution.py:486
  128.3 16.3 %finish.1.late = bf16[3,2048,256]{2,1,0:T(8,128)(2,1)S(1)} custom-call(bf16[3,2048,256]{2,1,0:T(8,128)(2,1)S(1)} %get-tuple-element.13.held, bf16[4,1024,256]{2,1,0:T(8,128)(2,1)S(1)} %get-tuple-element.14.far_late, f32[8,128]{1,0:T(8,128)} %get-tuple-element.16.token), custom_call_target="tpu_custom_call" | custom-call | tf_op jit(solution)/shard_map/finish/pallas_call | solution.py:495
  144.6 1.2 store_late.1

commit v13 on v12

--- a/solution.py
+++ b/solution.py
@@ -25,6 +25,7 @@
         self.me = lax.axis_index("tp")
         self.core = lax.rem(self.me, 2)
         self.row = self.me // 4
+        self.column = lax.rem(self.me // 2, 2)
         self.mate = self.me + 1 - 2 * self.core
         self.side = self.across(self.me)
         self.far = self.me + 2 - 4 * lax.rem(self.me // 2, 2)
@@ -101,7 +102,7 @@
     q_cols = pl.ds(pl.multiple_of(core * head, head), head)
     k_cols = pl.ds(pl.multiple_of(2 * head + core * part, part), part)
     v_cols = pl.ds(pl.multiple_of(3 * head + core * part, part), part)
-    lead = 6 * PIECE
+    lead = width // 4
     mine = (
         (wk_hbm, pl.ds(0, lead), k_cols),
         (wk_hbm, pl.ds(lead, width - lead), k_cols),
@@ -131,7 +132,18 @@
     across = send(detoured, w_far.at[mine[4][1], q_cols], across_send, across_recv, at.across(at.far))
 
     pl.semaphore_wait(barrier, 2 - core + at.row)
-    for load, copy in zip(load_w[:3], far_w[:3]):
+
+    @pl.when(at.column == 1)
+    def _():
+        send(wk_hbm.at[mine[0][1], :], w_far.at[mine[0][1], k_cols], fw_send.at[0], fw_recv.at[0], at.far).start()
+
+    load_w[0].wait()
+
+    @pl.when(at.column == 0)
+    def _():
+        far_w[0].start()
+
+    for load, copy in zip(load_w[1:3], far_w[1:3]):
         load.wait()
         copy.start()
     for load in load_w[3:]:

time: 146 us -> 146 us (level)
  no operation moved by 1% of the time
where the time goes in v13:
time: 146 us; the launch traced here: 145 us
  Pallas kernels  144 us (99%)
    pallas_call x1, Pallas kernels, local_step(): pl.pallas_call(gather, out_shape=[early, late, pltpu.VMEM((4, rows, head)...  123 us
    pallas_call x1, Pallas kernels, local_step(): pl.pallas_call(finish, out_shape=late, in_specs=[vmem] * 2 + [hbm], out_s...  16.4 us
    pallas_call x1, Pallas kernels, local_step(): pl.pallas_call(store_early, out_shape=final + [pltpu.HBM((8, 128), jnp.fl...  4.08 us

profile of v13, /device:TPU:1, one launch (start us, length us, event | category | flops | bytes accessed | tf_op | source)
XLA Modules:
  0.0 145.0 jit_solution(10918068892020671010)
XLA Ops:
  0.6 122.7 %gather.1 = (bf16[3,6144,256]{2,1,0:T(8,128)(2,1)S(1)}, bf16[3,2048,256]{2,1,0:T(8,128)(2,1)S(1)}, bf16[4,1024,256]{2,1,0:T(8,128)(2,1)S(1)}) custom-call(bf16[1024,2304]{1,0:T(8,128)(2,1)} %x_hbm.1, f32[2304]{0:T(1024)} %gain_hbm.1, bf16[2304,256]{1,0:T(8,128)(2,1)} %bitcast.7, bf16[2304,128]{1,0:T(8,128)(2,1)} %wk_hbm.1, bf16[2304,128]{1,0:T(8,128)(2,1)} %wv_hbm.1), custom_call_target="tpu_custom_call" | custom-call | tf_op jit(solution)/shard_map/gather/pallas_call | solution.py:476
  123.4 4.1 %store_early.1 = (bf16[8192,256]{1,0:T(8,128)(2,1)}, bf16[8192,256]{1,0:T(8,128)(2,1)}, bf16[8192,256]{1,0:T(8,128)(2,1)}, f32[8,128]{1,0:T(8,128)}) custom-call(bf16[3,6144,256]{2,1,0:T(8,128)(2,1)S(1)} %get-tuple-element.15.early, bf16[3,2048,256]{2,1,0:T(8,128)(2,1)S(1)} %get-tuple-element.13.held), custom_call_target="tpu_custom_call" | custom-call | tf_op jit(solution)/shard_map/store_early/pallas_call | solution.py:498
  127.5 16.4 %finish.1.late = bf16[3,2048,256]{2,1,0:T(8,128)(2,1)S(1)} custom-call(bf16[3,2048,256]{2,1,0:T(8,128)(2,1)S(1)} %get-tuple-element.13.held, bf16[4,1024,256]{2,1,0:T(8,128)(2,1)S(1)} %get-tuple-element.14.far_late, f32[8,128]{1,0:T(8,128)} %get-tuple-element.16.token), custom_call_target="tpu_custom_call" | custom-call | tf_op jit(solution)/shard_map/finish/pallas_call | solution.py:507
  143.8 1.2 store_late.1

commit v14 on v13

--- a/solution.py
+++ b/solution.py
@@ -62,12 +62,17 @@
         pl.when(at.core == core)(functools.partial(body, core))
 
 
-SAME, OTHER = range(2)
+SAME, OTHER, SAME_KV, SAME_Q = range(4)
 FIRST = (1, 3)
 
 
 def side_message(at, rows, stage, target, send_sem, recv_sem, kind, i, count=1):
-    src, dst, block, peer = ((KVQ, KVQ, LATE_FAR, at.far), (Q_OTHER, Q, LATE_FAR_MATE, at.far_mate))[kind]
+    src, dst, block, peer = {
+        SAME: (KVQ, KVQ, LATE_FAR, at.far),
+        SAME_KV: (KV, KV, LATE_FAR, at.far),
+        SAME_Q: (Q_SAME, Q, LATE_FAR, at.far),
+        OTHER: (Q_OTHER, Q, LATE_FAR_MATE, at.far_mate),
+    }[kind]
     return send(stage.at[src, span(i, CHUNK, 0, count), :], target.at[dst, span(i, CHUNK, block * rows, count), :], send_sem, recv_sem, peer)
 
 
@@ -355,7 +360,7 @@
     by_core(at, close)
 
 
-def finish(held, far_late, token, late, answer, send_sem, same_recv, other_recv, relay_recv):
+def finish(held, far_late, token, late, answer, send_sem, same_recv, lead_recv, rest_recv, relay_recv):
     rows = far_late.shape[1]
     chunks = rows // CHUNK
     at = Place()
@@ -368,32 +373,44 @@
         signal(barrier, at.far_mate)
 
     pl.semaphore_wait(barrier, 1 + 2 * at.core)
-    def message(kind, i, count):
-        return side_message(at, rows, far_late, late, send_sem, (same_recv, other_recv)[kind], kind, i, count)
+    def message(kind, recv_sem, i, count):
+        return side_message(at, rows, far_late, late, send_sem, recv_sem, kind, i, count)
 
     def relay(source, i, count):
         return late_relay(at, rows, source, late, send_sem, relay_recv, i, count)
 
+    def chunks_of_all(count):
+        ref = late.at[KVQ, span(0, CHUNK, 0, count), :]
+        return ref, ref
+
     def body(c):
         first, other_first = FIRST[c], FIRST[1 - c]
-        same, other = (message(kind, first, chunks - first) for kind in (SAME, OTHER))
-        same.start()
-        if c:
+        mine, others = chunks - first, chunks - other_first
+        if c == 0:
+            same = message(SAME, same_recv, first, mine)
+            same.start()
+            pl.semaphore_wait(answer, 2)
+            message(OTHER, lead_recv, first, 1).start()
+            message(OTHER, rest_recv, first + 1, mine - 1).start()
+        else:
+            same = message(SAME_KV, same_recv, first, mine)
+            same.start()
             signal(answer, at.mate)
             signal(answer, at.far_mate)
-        else:
-            pl.semaphore_wait(answer, 2)
-        other.start()
-        if c:
+            message(OTHER, rest_recv, first, mine).start()
             relay(held, 0, first).start()
         same.wait_recv()
-        relay(late, first, chunks - first).start()
-        arrived = chunks if c == 0 else chunks - other_first
-        relay(late, 0, arrived).wait_recv()
-        message(OTHER, other_first, chunks - other_first).wait_recv()
-        sent = 4 * (chunks - first) + 2 * (chunks if c else chunks - first)
-        everything = late.at[KVQ, span(0, CHUNK, 0, sent // 3), :]
-        pltpu.make_async_copy(everything, everything, send_sem).wait()
+        relay(late, first, mine).start()
+        if c == 1:
+            message(OTHER, lead_recv, other_first, 1).wait_recv()
+            message(SAME_Q, rest_recv, first, mine).start()
+        relay(late, 0, chunks if c == 0 else others).wait_recv()
+        if c == 0:
+            message(OTHER, rest_recv, other_first, others).wait_recv()
+        else:
+            pltpu.make_async_copy(*chunks_of_all((others - 1 + mine) // 3), rest_recv).wait()
+        sent = 4 * mine + 2 * (mine if c == 0 else chunks)
+        pltpu.make_async_copy(*chunks_of_all(sent // 3), send_sem).wait()
 
     by_core(at, body)
 
@@ -509,7 +526,7 @@
             out_shape=late,
             in_specs=[vmem] * 2 + [hbm],
             out_specs=vmem,
-            scratch_shapes=[pltpu.SemaphoreType.REGULAR] + [dma(())] * 4,
+            scratch_shapes=[pltpu.SemaphoreType.REGULAR] + [dma(())] * 5,
             compiler_params=small(collective_id=1, has_side_effects=True),
             name="finish",
         )(held, far_late, pltpu.with_memory_space_constraint(token, pltpu.HBM))

time: 146 us -> 146 us (level)
  no operation moved by 1% of the time
where the time goes in v14:
time: 146 us; the launch traced here: 145 us
  Pallas kernels  144 us (99%)
    pallas_call x1, Pallas kernels, local_step(): pl.pallas_call(gather, out_shape=[early, late, pltpu.VMEM((4, rows, head)...  123 us
    pallas_call x1, Pallas kernels, local_step(): pl.pallas_call(finish, out_shape=late, in_specs=[vmem] * 2 + [hbm], out_s...  16.4 us
    pallas_call x1, Pallas kernels, local_step(): pl.pallas_call(store_early, out_shape=final + [pltpu.HBM((8, 128), jnp.fl...  4.08 us

profile of v14, /device:TPU:1, one launch (start us, length us, event | category | flops | bytes accessed | tf_op | source)
XLA Modules:
  0.0 145.0 jit_solution(14439691976075664122)
XLA Ops:
  0.6 122.7 %gather.1 = (bf16[3,6144,256]{2,1,0:T(8,128)(2,1)S(1)}, bf16[3,2048,256]{2,1,0:T(8,128)(2,1)S(1)}, bf16[4,1024,256]{2,1,0:T(8,128)(2,1)S(1)}) custom-call(bf16[1024,2304]{1,0:T(8,128)(2,1)} %x_hbm.1, f32[2304]{0:T(1024)} %gain_hbm.1, bf16[2304,256]{1,0:T(8,128)(2,1)} %bitcast.7, bf16[2304,128]{1,0:T(8,128)(2,1)} %wk_hbm.1, bf16[2304,128]{1,0:T(8,128)(2,1)} %wv_hbm.1), custom_call_target="tpu_custom_call" | custom-call | tf_op jit(solution)/shard_map/gather/pallas_call | solution.py:493
  123.4 4.1 %store_early.1 = (bf16[8192,256]{1,0:T(8,128)(2,1)}, bf16[8192,256]{1,0:T(8,128)(2,1)}, bf16[8192,256]{1,0:T(8,128)(2,1)}, f32[8,128]{1,0:T(8,128)}) custom-call(bf16[3,6144,256]{2,1,0:T(8,128)(2,1)S(1)} %get-tuple-element.15.early, bf16[3,2048,256]{2,1,0:T(8,128)(2,1)S(1)} %get-tuple-element.13.held), custom_call_target="tpu_custom_call" | custom-call | tf_op jit(solution)/shard_map/store_early/pallas_call | solution.py:515
  127.5 16.4 %finish.1.late = bf16[3,2048,256]{2,1,0:T(8,128)(2,1)S(1)} custom-call(bf16[3,2048,256]{2,1,0:T(8,128)(2,1)S(1)} %get-tuple-element.13.held, bf16[4,1024,256]{2,1,0:T(8,128)(2,1)S(1)} %get-tuple-element.14.far_late, f32[8,128]{1,0:T(8,128)} %get-tuple-element.16.token), custom_call_target="tpu_custom_call" | custom-call | tf_op jit(solution)/shard_map/finish/pallas_call | solution.py:524
  143.8 1.2 store_late.1

commit v15 on v13

--- a/solution.py
+++ b/solution.py
@@ -11,7 +11,7 @@
 CHUNK = 256
 SIDE_CHUNK = 128
 PIECE = 16
-DETOUR = 32
+DETOUR = 48
 
 K, V, Q = range(3)
 KV, KVQ = pl.ds(0, 2), pl.ds(0, 3)

time: 146 us -> 145 us (level)
  no operation moved by 1% of the time
where the time goes in v15:
time: 145 us
  Pallas kernels  144 us (99%)
    pallas_call x1, Pallas kernels, local_step(): pl.pallas_call(gather, out_shape=[early, late, pltpu.VMEM((4, rows, head)...  123 us
    pallas_call x1, Pallas kernels, local_step(): pl.pallas_call(finish, out_shape=late, in_specs=[vmem] * 2 + [hbm], out_s...  16.4 us
    pallas_call x1, Pallas kernels, local_step(): pl.pallas_call(store_early, out_shape=final + [pltpu.HBM((8, 128), jnp.fl...  4.08 us

profile of v15, /device:TPU:1, one launch (start us, length us, event | category | flops | bytes accessed | tf_op | source)
XLA Modules:
  0.0 144.8 jit_solution(7703816618870455245)
XLA Ops:
  0.6 122.6 %gather.1 = (bf16[3,6144,256]{2,1,0:T(8,128)(2,1)S(1)}, bf16[3,2048,256]{2,1,0:T(8,128)(2,1)S(1)}, bf16[4,1024,256]{2,1,0:T(8,128)(2,1)S(1)}) custom-call(bf16[1024,2304]{1,0:T(8,128)(2,1)} %x_hbm.1, f32[2304]{0:T(1024)} %gain_hbm.1, bf16[2304,256]{1,0:T(8,128)(2,1)} %bitcast.7, bf16[2304,128]{1,0:T(8,128)(2,1)} %wk_hbm.1, bf16[2304,128]{1,0:T(8,128)(2,1)} %wv_hbm.1), custom_call_target="tpu_custom_call" | custom-call | tf_op jit(solution)/shard_map/gather/pallas_call | solution.py:476
  123.2 4.1 %store_early.1 = (bf16[8192,256]{1,0:T(8,128)(2,1)}, bf16[8192,256]{1,0:T(8,128)(2,1)}, bf16[8192,256]{1,0:T(8,128)(2,1)}, f32[8,128]{1,0:T(8,128)}) custom-call(bf16[3,6144,256]{2,1,0:T(8,128)(2,1)S(1)} %get-tuple-element.15.early, bf16[3,2048,256]{2,1,0:T(8,128)(2,1)S(1)} %get-tuple-element.13.held), custom_call_target="tpu_custom_call" | custom-call | tf_op jit(solution)/shard_map/store_early/pallas_call | solution.py:498
  127.3 16.4 %finish.1.late = bf16[3,2048,256]{2,1,0:T(8,128)(2,1)S(1)} custom-call(bf16[3,2048,256]{2,1,0:T(8,128)(2,1)S(1)} %get-tuple-element.13.held, bf16[4,1024,256]{2,1,0:T(8,128)(2,1)S(1)} %get-tuple-element.14.far_late, f32[8,128]{1,0:T(8,128)} %get-tuple-element.16.token), custom_call_target="tpu_custom_call" | custom-call | tf_op jit(solution)/shard_map/finish/pallas_call | solution.py:507
  143.6 1.2 store_late.1

commit v16 on v15

--- a/solution.py
+++ b/solution.py
@@ -137,11 +137,32 @@
     def _():
         send(wk_hbm.at[mine[0][1], :], w_far.at[mine[0][1], k_cols], fw_send.at[0], fw_recv.at[0], at.far).start()
 
-    load_w[0].wait()
-
     @pl.when(at.column == 0)
     def _():
+        load_w[0].wait()
         far_w[0].start()
+
+    @pl.when(core == 0)
+    def _():
+        signal(mate_answer, at.mate)
+
+    @pl.when(at.row == 1)
+    def _():
+        signal(side_answer, at.side)
+
+    @pl.when(core == 1)
+    def _():
+        pl.semaphore_wait(mate_answer, 1)
+
+    signal(far_answer, at.far)
+
+    @pl.when(at.row == 0)
+    def _():
+        pl.semaphore_wait(side_answer, 1)
+
+    @pl.when(at.column == 1)
+    def _():
+        load_w[0].wait()
 
     for load, copy in zip(load_w[1:3], far_w[1:3]):
         load.wait()
@@ -152,32 +173,15 @@
     @pl.when(at.row == 0)
     def _():
         far_w[3].start()
-
-    @pl.when(core == 0)
-    def _():
-        signal(mate_answer, at.mate)
-
-    @pl.when(at.row == 1)
-    def _():
-        signal(side_answer, at.side)
+        aside.start()
+
+    for copy in mate_w:
+        copy.start()
 
     gain_copy = pltpu.make_async_copy(gain_hbm, gain, load_gain)
     gain_copy.start()
     for i in range(chunks):
         load_chunk(i).start()
-
-    @pl.when(core == 1)
-    def _():
-        pl.semaphore_wait(mate_answer, 1)
-
-    signal(far_answer, at.far)
-    for copy in mate_w:
-        copy.start()
-
-    @pl.when(at.row == 0)
-    def _():
-        pl.semaphore_wait(side_answer, 1)
-        aside.start()
 
     loop(0, side_chunks, lambda i: side_chunk(i).start())
 

time: 145 us -> 145 us (level)
  no operation moved by 1% of the time
where the time goes in v16:
time: 145 us
  Pallas kernels  144 us (99%)
    pallas_call x1, Pallas kernels, local_step(): pl.pallas_call(gather, out_shape=[early, late, pltpu.VMEM((4, rows, head)...  123 us
    pallas_call x1, Pallas kernels, local_step(): pl.pallas_call(finish, out_shape=late, in_specs=[vmem] * 2 + [hbm], out_s...  16.4 us
    pallas_call x1, Pallas kernels, local_step(): pl.pallas_call(store_early, out_shape=final + [pltpu.HBM((8, 128), jnp.fl...  4.08 us

profile of v16, /device:TPU:1, one launch (start us, length us, event | category | flops | bytes accessed | tf_op | source)
XLA Modules:
  0.0 144.8 jit_solution(406163277440056926)
XLA Ops:
  0.6 122.6 %gather.1 = (bf16[3,6144,256]{2,1,0:T(8,128)(2,1)S(1)}, bf16[3,2048,256]{2,1,0:T(8,128)(2,1)S(1)}, bf16[4,1024,256]{2,1,0:T(8,128)(2,1)S(1)}) custom-call(bf16[1024,2304]{1,0:T(8,128)(2,1)} %x_hbm.1, f32[2304]{0:T(1024)} %gain_hbm.1, bf16[2304,256]{1,0:T(8,128)(2,1)} %bitcast.7, bf16[2304,128]{1,0:T(8,128)(2,1)} %wk_hbm.1, bf16[2304,128]{1,0:T(8,128)(2,1)} %wv_hbm.1), custom_call_target="tpu_custom_call" | custom-call | tf_op jit(solution)/shard_map/gather/pallas_call | solution.py:480
  123.2 4.1 %store_early.1 = (bf16[8192,256]{1,0:T(8,128)(2,1)}, bf16[8192,256]{1,0:T(8,128)(2,1)}, bf16[8192,256]{1,0:T(8,128)(2,1)}, f32[8,128]{1,0:T(8,128)}) custom-call(bf16[3,6144,256]{2,1,0:T(8,128)(2,1)S(1)} %get-tuple-element.15.early, bf16[3,2048,256]{2,1,0:T(8,128)(2,1)S(1)} %get-tuple-element.13.held), custom_call_target="tpu_custom_call" | custom-call | tf_op jit(solution)/shard_map/store_early/pallas_call | solution.py:502
  127.3 16.4 %finish.1.late = bf16[3,2048,256]{2,1,0:T(8,128)(2,1)S(1)} custom-call(bf16[3,2048,256]{2,1,0:T(8,128)(2,1)S(1)} %get-tuple-element.13.held, bf16[4,1024,256]{2,1,0:T(8,128)(2,1)S(1)} %get-tuple-element.14.far_late, f32[8,128]{1,0:T(8,128)} %get-tuple-element.16.token), custom_call_target="tpu_custom_call" | custom-call | tf_op jit(solution)/shard_map/finish/pallas_call | solution.py:511
  143.6 1.2 store_late.1

commit v17 on v16

--- a/solution.py
+++ b/solution.py
@@ -11,7 +11,7 @@
 CHUNK = 256
 SIDE_CHUNK = 128
 PIECE = 16
-DETOUR = 48
+DETOUR = 64
 
 K, V, Q = range(3)
 KV, KVQ = pl.ds(0, 2), pl.ds(0, 3)
@@ -30,7 +30,8 @@
         self.side = self.across(self.me)
         self.far = self.me + 2 - 4 * lax.rem(self.me // 2, 2)
         self.far_mate = self.far + 1 - 2 * self.core
-        self.first = FIRST[0] + (FIRST[1] - FIRST[0]) * self.core
+        self.turn = 1 - self.core
+        self.first = FIRST[0] + (FIRST[1] - FIRST[0]) * self.turn
         self.first_other = FIRST[0] + FIRST[1] - self.first
 
     def across(self, device):
@@ -57,9 +58,9 @@
     return pl.ds(pl.multiple_of(base + i * size, size), count * size)
 
 
-def by_core(at, body):
-    for core in range(2):
-        pl.when(at.core == core)(functools.partial(body, core))
+def by_turn(at, body):
+    for turn in range(2):
+        pl.when(at.turn == turn)(functools.partial(body, turn))
 
 
 SAME, OTHER = range(2)
@@ -298,7 +299,7 @@
 
         @pl.when(done & (n == at.first - 1))
         def _():
-            by_core(at, lambda c: message(SAME, 0, FIRST[c]).start())
+            by_turn(at, lambda c: message(SAME, 0, FIRST[c]).start())
 
     loop(0, side_chunks - 1, side_step)
 
@@ -356,7 +357,7 @@
             onward.wait_recv()
         same.wait_send()
 
-    by_core(at, close)
+    by_turn(at, close)
 
 
 def finish(held, far_late, token, late, answer, send_sem, same_recv, other_recv, relay_recv):
@@ -366,12 +367,12 @@
     barrier = pltpu.get_barrier_semaphore()
     signal(barrier, at.far)
 
-    @pl.when(at.core == 0)
+    @pl.when(at.turn == 0)
     def _():
         signal(barrier, at.mate)
         signal(barrier, at.far_mate)
 
-    pl.semaphore_wait(barrier, 1 + 2 * at.core)
+    pl.semaphore_wait(barrier, 1 + 2 * at.turn)
     def message(kind, i, count):
         return side_message(at, rows, far_late, late, send_sem, (same_recv, other_recv)[kind], kind, i, count)
 
@@ -399,7 +400,7 @@
         everything = late.at[KVQ, span(0, CHUNK, 0, sent // 3), :]
         pltpu.make_async_copy(everything, everything, send_sem).wait()
 
-    by_core(at, body)
+    by_turn(at, body)
 
 
 def late_chunks(core, held):
@@ -436,7 +437,7 @@
     rows = early.shape[1] // len(owners)
     outs = (k_out, v_out, q_out)
     for core in range(2):
-        @pl.when(at.core == core)
+        @pl.when(at.turn == core)
         def _():
             run([
                 pltpu.make_async_copy(early.at[o, pl.ds(block * rows, rows), :], out.at[span(owner, rows), :], sem)
@@ -448,7 +449,7 @@
 def store_late(late, q_in, k_in, v_in, q_out, k_out, v_out, sem):
     at = Place()
     for core in range(2):
-        @pl.when(at.core == core)
+        @pl.when(at.turn == core)
         def _():
             run(store_chunks(at, late, (k_out, v_out, q_out), sem, core, False))
 

time: 145 us -> 146 us (level)
    pallas_call x1, Pallas kernels: 123 us -> 113 us  [local_step(): pl.pallas_call(gather, out_shape=[early, late, pltpu.VMEM((4, rows, head)...]
    pallas_call x1, Pallas kernels: 16.4 us -> 25.6 us  [local_step(): pl.pallas_call(finish, out_shape=late, in_specs=[vmem] * 2 + [hbm], out_s...]
where the time goes in v17:
time: 146 us; the launch traced here: 145 us
  Pallas kernels  144 us (99%)
    pallas_call x1, Pallas kernels, local_step(): pl.pallas_call(gather, out_shape=[early, late, pltpu.VMEM((4, rows, head)...  113 us
    pallas_call x1, Pallas kernels, local_step(): pl.pallas_call(finish, out_shape=late, in_specs=[vmem] * 2 + [hbm], out_s...  25.6 us
    pallas_call x1, Pallas kernels, local_step(): pl.pallas_call(store_early, out_shape=final + [pltpu.HBM((8, 128), jnp.fl...  3.85 us

profile of v17, /device:TPU:1, one launch (start us, length us, event | category | flops | bytes accessed | tf_op | source)
XLA Modules:
  0.0 144.5 jit_solution(17424660658582506944)
XLA Ops:
  0.6 113.0 %gather.1 = (bf16[3,6144,256]{2,1,0:T(8,128)(2,1)S(1)}, bf16[3,2048,256]{2,1,0:T(8,128)(2,1)S(1)}, bf16[4,1024,256]{2,1,0:T(8,128)(2,1)S(1)}) custom-call(bf16[1024,2304]{1,0:T(8,128)(2,1)} %x_hbm.1, f32[2304]{0:T(1024)} %gain_hbm.1, bf16[2304,256]{1,0:T(8,128)(2,1)} %bitcast.7, bf16[2304,128]{1,0:T(8,128)(2,1)} %wk_hbm.1, bf16[2304,128]{1,0:T(8,128)(2,1)} %wv_hbm.1), custom_call_target="tpu_custom_call" | custom-call | tf_op jit(solution)/shard_map/gather/pallas_call | solution.py:481
  113.6 3.9 %store_early.1 = (bf16[8192,256]{1,0:T(8,128)(2,1)}, bf16[8192,256]{1,0:T(8,128)(2,1)}, bf16[8192,256]{1,0:T(8,128)(2,1)}, f32[8,128]{1,0:T(8,128)}) custom-call(bf16[3,6144,256]{2,1,0:T(8,128)(2,1)S(1)} %get-tuple-element.15.early, bf16[3,2048,256]{2,1,0:T(8,128)(2,1)S(1)} %get-tuple-element.13.held), custom_call_target="tpu_custom_call" | custom-call | tf_op jit(solution)/shard_map/store_early/pallas_call | solution.py:503
  117.5 25.6 %finish.1.late = bf16[3,2048,256]{2,1,0:T(8,128)(2,1)S(1)} custom-call(bf16[3,2048,256]{2,1,0:T(8,128)(2,1)S(1)} %get-tuple-element.13.held, bf16[4,1024,256]{2,1,0:T(8,128)(2,1)S(1)} %get-tuple-element.14.far_late, f32[8,128]{1,0:T(8,128)} %get-tuple-element.16.token), custom_call_target="tpu_custom_call" | custom-call | tf_op jit(solution)/shard_map/finish/pallas_call | solution.py:512
  143.1 1.4 store_late.1
